TPU v7x, 32 devices: a whole 2x2x4 slice. The times are simulated.
32 devices in a mesh: vocab: 16 (over z, y, x), width: 2 (over core).
Axes of the slice: x: 2, y: 2, z: 4, core: 2. Of those that a mesh axis runs over, the one named last changes fastest.
Arguments:
- token_grads: bfloat16 [16384, 4608], P('vocab', 'width'), may hold values from -6 to 6
- token_slot: int32 [16384], P('vocab'), may hold values from 0 to 255, as said below
- slot_rows: int32 [16, 256], P('vocab'), may hold values from 0 to 1023, as said below
- counts: int32 [16, 16], P('vocab'), may hold values from 1 to 16, as said below
- weights: bfloat16 [16384, 4608], P('vocab', 'width'), may hold values from -0.29882812 to 0.29882812
- moment: bfloat16 [16384, 4608], P('vocab', 'width'), may hold values from -2 to 2
- row_scale: float32 [16384], P('vocab'), may hold values from 0.1 to 4
- row_steps: int32 [16384], P('vocab'), may hold values from 0 to 11
Outputs:
- new_weights: bfloat16 [16384, 4608], P('vocab', 'width')
- new_moment: bfloat16 [16384, 4608], P('vocab', 'width')
- new_scale: float32 [16384], P('vocab')
Inputs may be any that keep to these rules, and one draw needn't show every extreme that they name: `token_slot`: each token names a live slot of its own source. `slot_rows`: within one source and one owner the 16 entries are distinct. `counts`: in every draw some owners receive 16 live slots from every source.
All inputs are finite; a program needn't handle non-finite values.
Results may differ from a plain program's by a relative error of at most 0.0011.
Values may be sent and summed in bfloat16 or wider, within the bound.
No kernel may reach another device: no remote copies, remote signals or barrier semaphores. Data moves between devices by JAX's collectives and lax.ppermute only.
A program may use at most 128 MiB of HBM per device.

v0:
```python
import jax
import jax.numpy as jnp
from jax import lax
from jax.sharding import PartitionSpec as P

D = 4608


def shards(token_grads, token_slot, slot_rows, counts, weights, moment, row_scale, row_steps):
    owners = lax.axis_size("vocab")
    slots_all = slot_rows.shape[1]
    cap = slots_all // owners
    half = token_grads.shape[1]
    rows_own = weights.shape[0]
    placing = token_slot[None, :] == jnp.arange(slots_all, dtype=jnp.int32)[:, None]
    slot_grads = jnp.dot(
        placing.astype(jnp.bfloat16), token_grads, preferred_element_type=jnp.float32
    ).astype(jnp.bfloat16)
    within = jnp.arange(cap, dtype=jnp.int32)
    live = within[None, :] < counts[0][:, None]
    named = jnp.where(live, slot_rows[0].reshape(owners, cap), -1)
    outgoing = slot_grads.reshape(owners, cap, half)
    received, received_rows = (
        lax.all_to_all(outgoing, "vocab", split_axis=0, concat_axis=0, tiled=True),
        lax.all_to_all(named, "vocab", split_axis=0, concat_axis=0, tiled=True),
    )
    flat = received.reshape(owners * cap, half)
    flat_rows = received_rows.reshape(owners * cap)
    target = jnp.where(flat_rows < 0, rows_own, flat_rows)
    grad = jax.ops.segment_sum(flat.astype(jnp.float32), target, num_segments=rows_own + 1)[
        :rows_own
    ]
    hits = jax.ops.segment_sum(jnp.ones_like(target), target, num_segments=rows_own + 1)[:rows_own]
    touched = hits > 0
    partial_sum = jnp.sum(grad * grad, axis=1)
    square = lax.psum(partial_sum, "width") / D
    step_count = (row_steps + 1).astype(jnp.float32)
    old_moment = moment.astype(jnp.float32)
    first = jnp.where(touched[:, None], 0.9 * old_moment + 0.1 * grad, old_moment)
    second = jnp.where(touched, 0.95 * row_scale + 0.05 * square, row_scale)
    fix_first = 1.0 - jnp.power(jnp.float32(0.9), step_count)
    fix_second = 1.0 - jnp.power(jnp.float32(0.95), step_count)
    denom = jnp.sqrt(second / fix_second) + 1e-08
    old = weights.astype(jnp.float32)
    stepped = old - 0.01 * (first / fix_first[:, None] / denom[:, None] + 0.1 * old)
    new_weights = jnp.where(touched[:, None], stepped, old).astype(jnp.bfloat16)
    return (new_weights, first.astype(jnp.bfloat16), second)


def solution(mesh):
    return jax.shard_map(
        shards,
        mesh=mesh,
        in_specs=(
            P("vocab", "width"),
            P("vocab"),
            P("vocab", None),
            P("vocab", None),
            P("vocab", "width"),
            P("vocab", "width"),
            P("vocab"),
            P("vocab"),
        ),
        out_specs=(P("vocab", "width"), P("vocab", "width"), P("vocab")),
        check_vma=False,
    )
```

profile of v0, /device:TPU:9, one launch (start us, length us, event | category | flops | bytes accessed | tf_op | source)
XLA Modules:
  0.0 80.1 jit_solution(982246932851753960)
XLA Ops:
  0.6 0.5 broadcast.73
  1.1 1.3 %reduce.6 = s32[256]{0:T(256)S(1)} reduce(s32[1,256]{1,0:T(1,128)} %param.10, s32[]{:T(128)} %broadcast.73), dimensions={0}, to_apply=%param.10.reduce_sub_computation.3 | reduce | bytes 2052 | tf_op args[2]
  2.5 0.1 reshape_squeeze.3
  2.6 1.3 %compare_select_fusion = s32[16,1,16]{2,1,0:T(1,128)} fusion(s32[16,1,16]{2,1,0:T(1,128)S(1)} %reshape_squeeze.3, s32[16]{0:T(128)} %bitcast.9), kind=kLoop, calls=%fused_computation.18 | loop fusion | flops 512 | bytes 2112 | tf_op jit(solution)/shard_map/jit(_where)/select_n | solution.py:21
  3.9 6.7 %all-to-all-start = ((s32[16,1,16]{2,1,0:T(1,128)}), s32[16,1,16]{2,1,0:T(1,128)S(1)}, u32[]{:S(2)}, u32[]{:S(2)}) async-start(s32[16,1,16]{2,1,0:T(1,128)} %compare_select_fusion), calls=%async_computation | async-start | bytes 16384 | tf_op jit(solution)/shard_map/all_to_all | solution.py:25
  10.6 4.8 %convolution_convert_fusion = bf16[256,2304]{1,0:T(8,128)(2,1)} fusion(bf16[1024,2304]{1,0:T(8,128)(2,1)} %param.8, s32[1024]{0:T(1024)} %param.9), kind=kOutput, calls=%fused_computation.13 | convolution fusion | flops 1208811520 | bytes 5902336 | tf_op jit(solution)/shard_map/dot_general | solution.py:16
  15.4 0.2 all-to-all-done
  15.6 6.1 %all-to-all-start.1 = ((bf16[16,16,2304]{2,1,0:T(8,128)(2,1)}), bf16[16,16,2304]{2,1,0:T(8,128)(2,1)S(1)}, u32[]{:S(2)}, u32[]{:S(2)}) async-start(bf16[16,16,2304]{2,1,0:T(8,128)(2,1)} %bitcast.2), calls=%async_computation.1 | async-start | bytes 2359296 | tf_op jit(solution)/shard_map/all_to_all | solution.py:24
  21.7 0.7 reduce.7
  22.4 0.1 reshape.89
  22.5 2.2 %scatter_custom_fusion = s32[1025]{0:T(1024)S(1)} fusion(s32[256]{0:T(256)S(1)} %bitcast.7, s32[256]{0:T(256)S(1)} %broadcast.57, s32[]{:T(128)} %constant.12.clone.1), kind=kCustom, calls=%fused_computation.23 | custom fusion | flops 256 | bytes 4104 | tf_op jit(solution)/shard_map/scatter-add | solution.py:33
  24.7 24.2 %all-to-all-done.1 = bf16[16,16,2304]{2,1,0:T(8,128)(2,1)S(1)} async-done(((bf16[16,16,2304]{2,1,0:T(8,128)(2,1)}), bf16[16,16,2304]{2,1,0:T(8,128)(2,1)S(1)}, u32[]{:S(2)}, u32[]{:S(2)}) %all-to-all-start.1) | async-done | bytes 1179680 | tf_op jit(solution)/shard_map/all_to_all | solution.py:24
  49.0 0.0 copy-start
  49.0 0.0 copy-start.1
  49.0 8.2 %scatter_custom_fusion.1 = f32[1025,2304]{1,0:T(8,128)} fusion(s32[256]{0:T(256)S(1)} %bitcast.8, f32[]{:T(128)} %constant.17.clone.1, bf16[256,2304]{1,0:T(8,128)(2,1)S(1)} %bitcast.6), kind=kCustom, calls=%fused_computation.11 | custom fusion | flops 1179648 | bytes 10626052 | tf_op jit(solution)/shard_map/scatter-add | solution.py:30
  57.2 4.4 %multiply_reduce_fusion = f32[1024]{0:T(1024)S(1)} fusion(f32[1025,2304]{1,0:T(8,128)} %scatter_custom_fusion.1), kind=kLoop, calls=%fused_computation.10 | loop fusion | flops 4717568 | bytes 9441280 | tf_op jit(solution)/shard_map/reduce_sum | solution.py:35
  61.5 4.6 %psum.7 = f32[1024]{0:T(1024)S(1)} all-reduce(f32[1024]{0:T(1024)S(1)} %multiply_reduce_fusion), channel_id=1, replica_groups=mesh['vocab'=16,'width'=2] {'width'}, use_global_device_ids=true, to_apply=%region_3.4 | all-reduce | flops 1024 | bytes 8192 | tf_op jit(solution)/shard_map/psum | solution.py:36
  66.1 0.0 copy-done
  66.1 0.0 copy-done.1
  66.1 0.6 add_multiply_fusion
  66.7 13.4 %fusion.7 = (bf16[1024,2304]{1,0:T(8,128)(2,1)}, bf16[1024,2304]{1,0:T(8,128)(2,1)}) fusion(f32[1025,2304]{1,0:T(8,128)} %scatter_custom_fusion.1, bf16[1024,2304]{1,0:T(8,128)(2,1)} %param.13, pred[1024]{0:T(1024)(128)(4,1)S(1)} %get-tuple-element.5, f32[1024]{0:T(1024)S(1)} %get-tuple-element.3, bf16[1024,2304]{1,0:T(8,128)(2,1)} %param.12), kind=kLoop, calls=%fused_computation.15 | loop fusion | flops 33030144 | bytes 28316672 | tf_op jit(solution)/shard_map/convert_element_type | solution.py:47
  (2 shorter events, 0.0 us)
Async XLA Ops:
  3.9 11.7 %all-to-all-start = ((s32[16,1,16]{2,1,0:T(1,128)}), s32[16,1,16]{2,1,0:T(1,128)S(1)}, u32[]{:S(2)}, u32[]{:S(2)}) async-start(s32[16,1,16]{2,1,0:T(1,128)} %compare_select_fusion), calls=%async_computation | async-start | bytes 16384 | tf_op jit(solution)/shard_map/all_to_all | solution.py:25
  15.6 33.4 %all-to-all-start.1 = ((bf16[16,16,2304]{2,1,0:T(8,128)(2,1)}), bf16[16,16,2304]{2,1,0:T(8,128)(2,1)S(1)}, u32[]{:S(2)}, u32[]{:S(2)}) async-start(bf16[16,16,2304]{2,1,0:T(8,128)(2,1)} %bitcast.2), calls=%async_computation.1 | async-start | bytes 2359296 | tf_op jit(solution)/shard_map/all_to_all | solution.py:24
  49.0 17.2 %copy-start = (s32[1024]{0:T(1024)S(1)}, s32[1024]{0:T(1024)}, u32[]{:S(2)}) copy-start(s32[1024]{0:T(1024)} %param.15) | copy-start | bytes 12292
  49.0 17.2 %copy-start.1 = (f32[1024]{0:T(1024)S(1)}, f32[1024]{0:T(1024)}, u32[]{:S(2)}) copy-start(f32[1024]{0:T(1024)} %param.14) | copy-start | bytes 12292
where the time goes:
time: 80.5 us; the launch traced here: 80.1 us
  other arithmetic  32.1 us (40%)
  waiting for transfers between devices  24.5 us (30%)
  starting transfers between devices  12.8 us (16%)
  matrix products  4.77 us (6%)
  blocking collectives  4.61 us (6%)
    all_to_all x1, waiting for transfers between devices, shards(): lax.all_to_all(outgoing, 'vocab', split_axis=0, concat_axis=0, tiled=True)  24.2 us
    convert_element_type x1, other arithmetic, shards(): return (new_weights, first.astype(jnp.bfloat16), second)  13.4 us
    scatter-add x1, other arithmetic, shards(): jax.ops.segment_sum(flat.astype(jnp.float32), target, num_segments=rows_o...  8.19 us
    all_to_all x1, starting transfers between devices, shards(): lax.all_to_all(named, 'vocab', split_axis=0, concat_axis=0, tiled=True)  6.66 us
    all_to_all x1, starting transfers between devices, shards(): lax.all_to_all(outgoing, 'vocab', split_axis=0, concat_axis=0, tiled=True)  6.13 us
    dot_general x1, matrix products, shards(): jnp.dot(placing.astype(jnp.bfloat16), token_grads, preferred_element_type...  4.77 us
    psum x1, blocking collectives, shards(): square = lax.psum(partial_sum, 'width') / D  4.61 us
    reduce_sum x1, other arithmetic, shards(): partial_sum = jnp.sum(grad * grad, axis=1)  4.36 us
  transfers between devices with their start and end apart: 2, of which 2 were waited for; matrix products, arithmetic and copies ran while one was open for 10% of the time, Pallas kernels for 0%

commit v1 on v0

v1 whole, which is shorter than its diff:
```python
import functools

import jax
import jax.numpy as jnp
from jax import lax
from jax.experimental import pallas as pl
from jax.experimental.pallas import tpu as pltpu
from jax.sharding import PartitionSpec as P


LANES = 128
MIB = 1 << 20
VMEM = pl.BlockSpec(memory_space=pltpu.VMEM)
SMEM = pl.BlockSpec(memory_space=pltpu.SMEM)
ANY = pl.BlockSpec(memory_space=pl.ANY)
F32, BF16, I32 = jnp.float32, jnp.bfloat16, jnp.int32


def iota(shape, axis):
    return lax.broadcasted_iota(I32, shape, axis)


def name_rows(slots):
    return -(-2 * (slots // LANES) // 8) * 8


def col_step(half):
    return 2 * LANES if half % (2 * LANES) == 0 else LANES


def send_kernel(
    owners, cap, me_ref, counts_far, slot_far, rows_far, grads_ref, *rest
):
    outs, rest = rest[:owners], rest[owners:]
    onehot, buf, counts_ref, slot_ref, rows_ref, sems, small = rest
    tokens, half = grads_ref.shape
    slots = owners * cap
    step = col_step(half)
    copies = [
        pltpu.make_async_copy(
            grads_ref.at[:, pl.ds(c, step)], buf.at[:, pl.ds(c, step)], sems.at[c // step]
        )
        for c in range(0, half, step)
    ]
    arrivals = [
        pltpu.make_async_copy(far, ref, small.at[i])
        for i, (far, ref) in enumerate(
            ((slot_far, slot_ref), (rows_far, rows_ref), (counts_far, counts_ref))
        )
    ]
    for copy in arrivals + copies:
        copy.start()
    for copy in arrivals:
        copy.wait()
    me = me_ref[0]
    groups = slots // LANES
    turned = jnp.bitwise_xor(slot_ref[...], me * cap)
    for t in range(tokens // LANES):
        hit = turned[t : t + 1, :] == iota((slots, LANES), 0)
        onehot[:, t * LANES : (t + 1) * LANES] = jnp.where(hit, 1.0, 0.0).astype(BF16)
    lane = iota((1, slots), 1)
    owner, within = lane // cap, lax.rem(lane, cap)
    live = jnp.zeros((1, slots), I32)
    for o in range(owners):
        live = jnp.where((owner == o) & (within < counts_ref[0, o]), 1, live)
    rows = rows_ref[...]
    high = (rows // LANES + 1) * live
    low = lax.rem(rows, LANES) * live
    digits = jnp.concatenate(
        [high.astype(F32), low.astype(F32), jnp.zeros((6, slots), F32)], axis=0
    ).astype(BF16)
    turn = jnp.where(
        iota((slots, slots), 0) == jnp.bitwise_xor(iota((slots, slots), 1), me * cap), 1.0, 0.0
    ).astype(BF16)
    digits = jnp.dot(digits, turn, preferred_element_type=F32)
    pad = name_rows(slots) - 2 * groups
    names = [digits[0:1, g * LANES : (g + 1) * LANES] for g in range(groups)]
    names += [digits[1:2, g * LANES : (g + 1) * LANES] for g in range(groups)]
    if pad:
        names.append(jnp.zeros((pad, LANES), F32))
    names = jnp.concatenate(names, axis=0)
    base = half // LANES * cap
    sub, at = iota(names.shape, 0), iota(names.shape, 1)
    place = (lax.rem(sub, groups) * LANES + at) // cap
    for d in range(owners):
        outs[d][base:, :] = jnp.where(place == d, names, 0.0).astype(BF16)
    for c in range(0, half, step):
        copies[c // step].wait()
        got = jnp.dot(onehot[...], buf[:, c : c + step], preferred_element_type=F32).astype(BF16)
        for d in range(owners):
            for t in range(step // LANES):
                row = (c // LANES + t) * cap
                outs[d][row : row + cap, :] = got[
                    d * cap : (d + 1) * cap, t * LANES : (t + 1) * LANES
                ]


def grad_kernel(owners, cap, *refs):
    blocks = refs[:owners]
    grad_ref, squares_ref, hits_ref, count_ref, place, acc = refs[owners:]
    rows, half = grad_ref.shape
    slots = owners * cap
    groups = slots // LANES
    step = col_step(half)
    base = half // LANES * cap
    names = blocks[0][base:, :].astype(F32)
    for d in range(1, owners):
        names = names + blocks[d][base:, :].astype(F32)
    names = names.astype(I32)
    for g in range(groups):
        row = (names[g : g + 1, :] - 1) * LANES + names[groups + g : groups + g + 1, :]
        hit = row == iota((rows, LANES), 0)
        place[:, g * LANES : (g + 1) * LANES] = jnp.where(hit, 1.0, 0.0).astype(BF16)
    count_ref[...] = jnp.dot(
        place[...], jnp.ones((slots, LANES), BF16), preferred_element_type=F32
    )
    for c in range(0, half, step):
        parts = []
        for t in range(step // LANES):
            at = (c // LANES + t) * cap
            parts.append(jnp.concatenate([b[at : at + cap, :] for b in blocks], axis=0))
        got = jnp.concatenate(parts, axis=1) if len(parts) > 1 else parts[0]
        grad_ref[:, c : c + step] = jnp.dot(place[...], got, preferred_element_type=F32)
        for r in range(0, rows, LANES):
            total = acc[r : r + LANES, :] if c else None
            for t in range(step // LANES):
                x = grad_ref[r : r + LANES, c + t * LANES : c + (t + 1) * LANES]
                total = x * x if total is None else total + x * x
            acc[r : r + LANES, :] = total
    one = jnp.ones((8, LANES), F32)
    lanes = (((1,), (1,)), ((), ()))
    for r in range(rows // LANES):
        part = slice(r * LANES, (r + 1) * LANES)
        squares_ref[r : r + 1, :] = lax.dot_general(
            one, acc[part, :], lanes, precision=lax.Precision.HIGHEST, preferred_element_type=F32
        )[0:1, :]
        hits_ref[r : r + 1, :] = lax.dot_general(
            one, count_ref[part, :], lanes, precision=lax.Precision.HIGHEST, preferred_element_type=F32
        )[0:1, :]


def moment_kernel(grad_ref, count_ref, moment_ref, first_ref, new_ref, staged, sems):
    rows, half = grad_ref.shape
    strip = 16

    def copy(i):
        part = pl.ds(pl.multiple_of(i * LANES, LANES), LANES)
        return pltpu.make_async_copy(staged.at[part, :], new_ref.at[part, :], sems.at[i])

    @pl.loop(0, rows // LANES)
    def _(i):
        @pl.loop(0, LANES // strip)
        def _(j):
            part = pl.ds(pl.multiple_of(i * LANES + j * strip, strip), strip)
            keep = jnp.where(count_ref[part, :] > 0.0, 0.9, 1.0)
            for c in range(0, half, LANES):
                old = moment_ref[part, c : c + LANES].astype(F32)
                first = keep * old + 0.1 * grad_ref[part, c : c + LANES]
                first_ref[part, c : c + LANES] = first
                staged[part, c : c + LANES] = first.astype(BF16)

        copy(i).start()

    @pl.loop(0, rows // LANES)
    def _(i):
        copy(i).wait()


def weights_kernel(
    width, first_ref, weights_ref, mine_ref, other_ref, hits_ref, scale_ref, steps_ref,
    new_ref, new_scale_ref, staged, rates, sems,
):
    rows, half = first_ref.shape
    square = (mine_ref[...] + other_ref[...]) / width
    touched = hits_ref[...] > 0.5
    scale = scale_ref[...]
    second = jnp.where(touched, 0.95 * scale + 0.05 * square, scale)
    new_scale_ref[...] = second
    steps = (steps_ref[...] + 1).astype(F32)
    fix_first = 1.0 - jnp.exp(steps * jnp.log(jnp.float32(0.9)))
    fix_second = 1.0 - jnp.exp(steps * jnp.log(jnp.float32(0.95)))
    denom = jnp.sqrt(second / fix_second) + 1e-08
    rate = jnp.where(touched, 0.01 / (fix_first * denom), -1.0)
    eye = iota((LANES, LANES), 0) == iota((LANES, LANES), 1)
    for i in range(rows // LANES):
        column = jnp.sum(jnp.where(eye, rate[i : i + 1, :], 0.0), axis=1, keepdims=True)
        rates[i * LANES : (i + 1) * LANES, :] = jnp.broadcast_to(column, (LANES, LANES))
    strip = 16

    def copy(i):
        part = pl.ds(pl.multiple_of(i * LANES, LANES), LANES)
        return pltpu.make_async_copy(staged.at[part, :], new_ref.at[part, :], sems.at[i])

    @pl.loop(0, rows // LANES)
    def _(i):
        @pl.loop(0, LANES // strip)
        def _(j):
            part = pl.ds(pl.multiple_of(i * LANES + j * strip, strip), strip)
            rate = rates[part, :]
            keep = jnp.where(rate < 0.0, 1.0, 0.999)
            rate = jnp.maximum(rate, 0.0)
            for c in range(0, half, LANES):
                old = weights_ref[part, c : c + LANES].astype(F32)
                new = keep * old - rate * first_ref[part, c : c + LANES]
                staged[part, c : c + LANES] = new.astype(BF16)

        copy(i).start()

    @pl.loop(0, rows // LANES)
    def _(i):
        copy(i).wait()


def near(x):
    return pltpu.with_memory_space_constraint(x, pltpu.VMEM)


def far(x):
    return pltpu.with_memory_space_constraint(x, pltpu.HBM)


def params(limit):
    return pltpu.CompilerParams(vmem_limit_bytes=limit * MIB)


def shards(token_grads, token_slot, slot_rows, counts, weights, moment, row_scale, row_steps):
    owners = lax.axis_size("vocab")
    halves = lax.axis_size("width")
    slots = slot_rows.shape[1]
    cap = slots // owners
    tokens, half = token_grads.shape
    rows = weights.shape[0]
    assert owners & (owners - 1) == 0 and cap & (cap - 1) == 0
    assert rows % LANES == 0 and tokens % LANES == 0 and slots % LANES == 0 and half % LANES == 0
    me = lax.axis_index("vocab").astype(I32).reshape(1)
    height = half // LANES * cap + name_rows(slots)
    step = col_step(half)
    block = jax.ShapeDtypeStruct((height, LANES), BF16)
    outgoing = pl.pallas_call(
        functools.partial(send_kernel, owners, cap),
        out_shape=[block] * owners,
        in_specs=[SMEM, ANY, ANY, ANY, ANY],
        out_specs=[VMEM] * owners,
        scratch_shapes=[
            pltpu.VMEM((slots, tokens), BF16),
            pltpu.VMEM((tokens, half), BF16),
            pltpu.SMEM((1, owners), I32),
            pltpu.VMEM((tokens // LANES, LANES), I32),
            pltpu.VMEM((1, slots), I32),
            pltpu.SemaphoreType.DMA((half // step,)),
            pltpu.SemaphoreType.DMA((3,)),
        ],
        compiler_params=params(24),
        cost_estimate=pl.CostEstimate(
            flops=2 * slots * tokens * half, bytes_accessed=tokens * half * 2, transcendentals=0
        ),
        name="send",
    )(
        me, far(counts), far(token_slot.reshape(tokens // LANES, LANES)), far(slot_rows),
        far(token_grads),
    )
    received = {0: outgoing[0]}
    for d in range(1, owners):
        received[d] = lax.ppermute(outgoing[d], "vocab", [(s, s ^ d) for s in range(owners)])
    lined = jax.ShapeDtypeStruct((rows // LANES, LANES), F32)
    grad, squares, hits, count = pl.pallas_call(
        functools.partial(grad_kernel, owners, cap),
        out_shape=[pltpu.VMEM((rows, half), F32), lined, lined, pltpu.VMEM((rows, LANES), F32)],
        in_specs=[VMEM] * owners,
        out_specs=[VMEM] * 4,
        scratch_shapes=[pltpu.VMEM((rows, slots), BF16), pltpu.VMEM((rows, LANES), F32)],
        compiler_params=params(12),
        cost_estimate=pl.CostEstimate(
            flops=2 * slots * rows * half, bytes_accessed=slots * half * 2, transcendentals=0
        ),
        name="grad",
    )(*[received[d] for d in range(owners)])
    other = lax.ppermute(squares, "width", [(s, halves - 1 - s) for s in range(halves)])
    first, new_moment = pl.pallas_call(
        moment_kernel,
        out_shape=[pltpu.VMEM((rows, half), F32), jax.ShapeDtypeStruct((rows, half), BF16)],
        in_specs=[VMEM] * 3,
        out_specs=[VMEM, ANY],
        scratch_shapes=[pltpu.VMEM((rows, half), BF16), pltpu.SemaphoreType.DMA((rows // LANES,))],
        compiler_params=params(16),
        cost_estimate=pl.CostEstimate(flops=10**9, bytes_accessed=2 * rows * half, transcendentals=0),
        name="moment",
    )(near(grad), near(count), near(moment))
    new_weights, new_scale = pl.pallas_call(
        functools.partial(weights_kernel, halves * half),
        out_shape=[jax.ShapeDtypeStruct((rows, half), BF16), lined],
        in_specs=[VMEM] * 7,
        out_specs=[ANY, VMEM],
        scratch_shapes=[pltpu.VMEM((rows, half), BF16), pltpu.VMEM((rows, LANES), F32), pltpu.SemaphoreType.DMA((rows // LANES,))],
        compiler_params=params(16),
        name="weights",
    )(
        near(first), near(weights), squares, other, hits,
        row_scale.reshape(rows // LANES, LANES), row_steps.reshape(rows // LANES, LANES),
    )
    return new_weights, new_moment, new_scale.reshape(rows)


def solution(mesh):
    return jax.shard_map(
        shards,
        mesh=mesh,
        in_specs=(
            P("vocab", "width"),
            P("vocab"),
            P("vocab", None),
            P("vocab", None),
            P("vocab", "width"),
            P("vocab", "width"),
            P("vocab"),
            P("vocab"),
        ),
        out_specs=(P("vocab", "width"), P("vocab", "width"), P("vocab")),
        check_vma=False,
    )
```

time: 80.5 us -> 57.3 us (0.71)
  the two profiles are of different devices: /device:TPU:9 before, /device:TPU:1 now
where the time goes in v1:
time: 57.3 us; the launch traced here: 57.1 us
  starting transfers between devices  31.3 us (55%)
  Pallas kernels  15.9 us (28%)
  waiting for transfers between devices  9.19 us (16%)
  between operations  0.76 us (1%)
    ppermute x15, starting transfers between devices, shards(): lax.ppermute(outgoing[d], 'vocab', [(s, s ^ d) for s in range(owners)])  30 us
    ppermute x15, waiting for transfers between devices, shards(): lax.ppermute(outgoing[d], 'vocab', [(s, s ^ d) for s in range(owners)])  9.19 us
    pallas_call x1, Pallas kernels, shards(): pl.pallas_call(functools.partial(send_kernel, owners, cap), out_shape=[bl...  6.06 us
    pallas_call x1, Pallas kernels, shards(): pl.pallas_call(functools.partial(weights_kernel, halves * half), out_shap...  3.75 us
    pallas_call x1, Pallas kernels, shards(): pl.pallas_call(functools.partial(grad_kernel, owners, cap), out_shape=[pl...  3.17 us
    pallas_call x1, Pallas kernels, shards(): pl.pallas_call(moment_kernel, out_shape=[pltpu.VMEM((rows, half), F32), j...  2.87 us
    ppermute x1, starting transfers between devices, shards(): lax.ppermute(squares, 'width', [(s, halves - 1 - s) for s in range(halves)])  1.29 us
  transfers between devices with their start and end apart: 16, of which 2 were waited for; matrix products, arithmetic and copies ran while one was open for 0% of the time, Pallas kernels for 5%

profile of v1, /device:TPU:1, one launch (start us, length us, event | category | flops | bytes accessed | tf_op | source)
XLA Modules:
  0.0 57.1 jit_solution(5537694552228092854)
XLA Ops:
  0.6 0.0 slice-start
  0.6 0.0 slice-start.1
  0.7 6.1 %send.1 = (bf16[296,128]{1,0:T(8,128)(2,1)S(1)}, bf16[296,128]{1,0:T(8,128)(2,1)S(1)}, bf16[296,128]{1,0:T(8,128)(2,1)S(1)}, bf16[296,128]{1,0:T(8,128)(2,1)S(1)...) custom-call(s32[1]{0:T(128)} %bitcast.me_ref, ...), custom_call_target="tpu_custom_call" | custom-call | flops 1207959552 | bytes 4718592 | tf_op jit(solution)/shard_map/send/pallas_call | solution.py:239
  6.7 2.1 %collective-permute-start = (bf16[296,128]{1,0:T(8,128)(2,1)S(1)}, bf16[296,128]{1,0:T(8,128)(2,1)S(1)}, u32[]{:S(2)}, u32[]{:S(2)}) collective-permute-start(bf16[296,128]{1,0:T(8,128)(2,1)S(1)} %get-tuple-element.28), channel_id=1, source_target_pairs={{0,2},{2,0},{4,6},{6,4},{8,10},{10,8},{12,14},{14,12},{16,18},{18,... | collective-permute-start | bytes 227336 | tf_op jit(solution)/shard_map/ppermute | solution.py:264
  8.8 1.2 %collective-permute-start.1 = (bf16[296,128]{1,0:T(8,128)(2,1)S(1)}, bf16[296,128]{1,0:T(8,128)(2,1)S(1)}, u32[]{:S(2)}, u32[]{:S(2)}) collective-permute-start(bf16[296,128]{1,0:T(8,128)(2,1)S(1)} %get-tuple-element.29), channel_id=1, source_target_pairs={{0,4},{2,6},{4,0},{6,2},{8,12},{10,14},{12,8},{14,10},{16,20},{18,... | collective-permute-start | bytes 227336 | tf_op jit(solution)/shard_map/ppermute | solution.py:264
  10.1 2.2 %collective-permute-start.10 = (bf16[296,128]{1,0:T(8,128)(2,1)S(1)}, bf16[296,128]{1,0:T(8,128)(2,1)S(1)}, u32[]{:S(2)}, u32[]{:S(2)}) collective-permute-start(bf16[296,128]{1,0:T(8,128)(2,1)S(1)} %get-tuple-element.38), channel_id=1, source_target_pairs={{0,22},{2,20},{4,18},{6,16},{8,30},{10,28},{12,26},{14,24},{16,6},... | collective-permute-start | bytes 227336 | tf_op jit(solution)/shard_map/ppermute | solution.py:264
  12.3 1.1 %collective-permute-start.11 = (bf16[296,128]{1,0:T(8,128)(2,1)S(1)}, bf16[296,128]{1,0:T(8,128)(2,1)S(1)}, u32[]{:S(2)}, u32[]{:S(2)}) collective-permute-start(bf16[296,128]{1,0:T(8,128)(2,1)S(1)} %get-tuple-element.39), channel_id=1, source_target_pairs={{0,24},{2,26},{4,28},{6,30},{8,16},{10,18},{12,20},{14,22},{16,8},... | collective-permute-start | bytes 227336 | tf_op jit(solution)/shard_map/ppermute | solution.py:264
  13.4 3.1 %collective-permute-start.12 = (bf16[296,128]{1,0:T(8,128)(2,1)S(1)}, bf16[296,128]{1,0:T(8,128)(2,1)S(1)}, u32[]{:S(2)}, u32[]{:S(2)}) collective-permute-start(bf16[296,128]{1,0:T(8,128)(2,1)S(1)} %get-tuple-element.40), channel_id=1, source_target_pairs={{0,26},{2,24},{4,30},{6,28},{8,18},{10,16},{12,22},{14,20},{16,10}... | collective-permute-start | bytes 227336 | tf_op jit(solution)/shard_map/ppermute | solution.py:264
  16.5 0.0 collective-permute-done.refs_1_
  16.5 2.0 %collective-permute-start.13 = (bf16[296,128]{1,0:T(8,128)(2,1)S(1)}, bf16[296,128]{1,0:T(8,128)(2,1)S(1)}, u32[]{:S(2)}, u32[]{:S(2)}) collective-permute-start(bf16[296,128]{1,0:T(8,128)(2,1)S(1)} %get-tuple-element.41), channel_id=1, source_target_pairs={{0,28},{2,30},{4,24},{6,26},{8,20},{10,22},{12,16},{14,18},{16,12}... | collective-permute-start | bytes 227336 | tf_op jit(solution)/shard_map/ppermute | solution.py:264
  18.5 0.0 collective-permute-done.1.refs_2_
  18.5 2.1 %collective-permute-start.14 = (bf16[296,128]{1,0:T(8,128)(2,1)S(1)}, bf16[296,128]{1,0:T(8,128)(2,1)S(1)}, u32[]{:S(2)}, u32[]{:S(2)}) collective-permute-start(bf16[296,128]{1,0:T(8,128)(2,1)S(1)} %get-tuple-element.42), channel_id=1, source_target_pairs={{0,30},{2,28},{4,26},{6,24},{8,22},{10,20},{12,18},{14,16},{16,14}... | collective-permute-start | bytes 227336 | tf_op jit(solution)/shard_map/ppermute | solution.py:264
  20.6 0.0 collective-permute-done.10.refs_11_
  20.6 2.2 %collective-permute-start.2 = (bf16[296,128]{1,0:T(8,128)(2,1)S(1)}, bf16[296,128]{1,0:T(8,128)(2,1)S(1)}, u32[]{:S(2)}, u32[]{:S(2)}) collective-permute-start(bf16[296,128]{1,0:T(8,128)(2,1)S(1)} %get-tuple-element.30), channel_id=1, source_target_pairs={{0,6},{2,4},{4,2},{6,0},{8,14},{10,12},{12,10},{14,8},{16,22},{18,... | collective-permute-start | bytes 227336 | tf_op jit(solution)/shard_map/ppermute | solution.py:264
  22.8 0.0 collective-permute-done.11.refs_12_
  22.8 0.3 collective-permute-start.3
  23.1 0.0 collective-permute-done.12.refs_13_
  23.1 4.4 %collective-permute-start.4 = (bf16[296,128]{1,0:T(8,128)(2,1)S(1)}, bf16[296,128]{1,0:T(8,128)(2,1)S(1)}, u32[]{:S(2)}, u32[]{:S(2)}) collective-permute-start(bf16[296,128]{1,0:T(8,128)(2,1)S(1)} %get-tuple-element.32), channel_id=1, source_target_pairs={{0,10},{2,8},{4,14},{6,12},{8,2},{10,0},{12,6},{14,4},{16,26},{18,... | collective-permute-start | bytes 227336 | tf_op jit(solution)/shard_map/ppermute | solution.py:264
  27.5 0.0 collective-permute-done.13.refs_14_
  27.5 1.9 %collective-permute-start.5 = (bf16[296,128]{1,0:T(8,128)(2,1)S(1)}, bf16[296,128]{1,0:T(8,128)(2,1)S(1)}, u32[]{:S(2)}, u32[]{:S(2)}) collective-permute-start(bf16[296,128]{1,0:T(8,128)(2,1)S(1)} %get-tuple-element.33), channel_id=1, source_target_pairs={{0,12},{2,14},{4,8},{6,10},{8,4},{10,6},{12,0},{14,2},{16,28},{18,... | collective-permute-start | bytes 227336 | tf_op jit(solution)/shard_map/ppermute | solution.py:264
  29.4 0.0 collective-permute-done.14.refs_15_
  29.4 2.7 %collective-permute-start.6 = (bf16[296,128]{1,0:T(8,128)(2,1)S(1)}, bf16[296,128]{1,0:T(8,128)(2,1)S(1)}, u32[]{:S(2)}, u32[]{:S(2)}) collective-permute-start(bf16[296,128]{1,0:T(8,128)(2,1)S(1)} %get-tuple-element.34), channel_id=1, source_target_pairs={{0,14},{2,12},{4,10},{6,8},{8,6},{10,4},{12,2},{14,0},{16,30},{18,... | collective-permute-start | bytes 227336 | tf_op jit(solution)/shard_map/ppermute | solution.py:264
  32.1 0.0 collective-permute-done.2.refs_3_
  32.1 2.4 %collective-permute-start.7 = (bf16[296,128]{1,0:T(8,128)(2,1)S(1)}, bf16[296,128]{1,0:T(8,128)(2,1)S(1)}, u32[]{:S(2)}, u32[]{:S(2)}) collective-permute-start(bf16[296,128]{1,0:T(8,128)(2,1)S(1)} %get-tuple-element.35), channel_id=1, source_target_pairs={{0,16},{2,18},{4,20},{6,22},{8,24},{10,26},{12,28},{14,30},{16,0},... | collective-permute-start | bytes 227336 | tf_op jit(solution)/shard_map/ppermute | solution.py:264
  34.5 0.0 collective-permute-done.3.refs_4_
  34.5 1.2 %collective-permute-start.8 = (bf16[296,128]{1,0:T(8,128)(2,1)S(1)}, bf16[296,128]{1,0:T(8,128)(2,1)S(1)}, u32[]{:S(2)}, u32[]{:S(2)}) collective-permute-start(bf16[296,128]{1,0:T(8,128)(2,1)S(1)} %get-tuple-element.36), channel_id=1, source_target_pairs={{0,18},{2,16},{4,22},{6,20},{8,26},{10,24},{12,30},{14,28},{16,2},... | collective-permute-start | bytes 227336 | tf_op jit(solution)/shard_map/ppermute | solution.py:264
  35.7 0.0 collective-permute-done.4.refs_5_
  35.7 1.1 %collective-permute-start.9 = (bf16[296,128]{1,0:T(8,128)(2,1)S(1)}, bf16[296,128]{1,0:T(8,128)(2,1)S(1)}, u32[]{:S(2)}, u32[]{:S(2)}) collective-permute-start(bf16[296,128]{1,0:T(8,128)(2,1)S(1)} %get-tuple-element.37), channel_id=1, source_target_pairs={{0,20},{2,22},{4,16},{6,18},{8,28},{10,30},{12,24},{14,26},{16,4},... | collective-permute-start | bytes 227336 | tf_op jit(solution)/shard_map/ppermute | solution.py:264
  36.8 0.0 collective-permute-done.5.refs_6_
  36.8 0.0 collective-permute-done.6.refs_7_
  36.8 0.0 collective-permute-done.7.refs_8_
  36.8 8.0 %collective-permute-done.8.refs_9_ = bf16[296,128]{1,0:T(8,128)(2,1)S(1)} collective-permute-done((bf16[296,128]{1,0:T(8,128)(2,1)S(1)}, bf16[296,128]{1,0:T(8,128)(2,1)S(1)}, u32[]{:S(2)}, u32[]{:S(2)}) %collective-permute-start.8) | collective-permute-done | bytes 75808 | tf_op jit(solution)/shard_map/ppermute | solution.py:264
  44.8 1.2 %collective-permute-done.9.refs_10_ = bf16[296,128]{1,0:T(8,128)(2,1)S(1)} collective-permute-done((bf16[296,128]{1,0:T(8,128)(2,1)S(1)}, bf16[296,128]{1,0:T(8,128)(2,1)S(1)}, u32[]{:S(2)}, u32[]{:S(2)}) %collective-permute-start.9) | collective-permute-done | bytes 75808 | tf_op jit(solution)/shard_map/ppermute | solution.py:264
  45.9 0.0 slice-start.2
  45.9 3.2 %grad.1 = (f32[1024,2304]{1,0:T(8,128)S(1)}, f32[8,128]{1,0:T(8,128)S(1)}, f32[8,128]{1,0:T(8,128)S(1)}, f32[1024,128]{1,0:T(8,128)S(1)}) custom-call(bf16[296,128]{1,0:T(8,128)(2,1)S(1)} %get-tuple-element.27.refs_0_, bf16[296,128]{1,0:T(8,128)(2,1)S(1)} %collective-permute-done.refs_1_, bf16[296,128]{1,0:T(8,128)(2,1)S(1)} %collective-permute-done.1.refs_2_, ...), custom_call_target="tpu_custom_call" | custom-call | flops 1207959552 | bytes 1179648 | tf_op jit(solution)/shard_map/grad/pallas_call | solution.py:266
  49.1 1.3 %collective-permute-start.15 = (f32[8,128]{1,0:T(8,128)S(1)}, f32[8,128]{1,0:T(8,128)S(1)}, u32[]{:S(2)}, u32[]{:S(2)}) collective-permute-start(f32[8,128]{1,0:T(8,128)S(1)} %get-tuple-element.46.mine_ref), channel_id=1, source_target_pairs={{0,1},{1,0},{2,3},{3,2},{4,5},{5,4},{6,7},{7,6},{8,9},{9,8},{10,11... | collective-permute-start | bytes 12296 | tf_op jit(solution)/shard_map/ppermute | solution.py:278
  50.4 0.0 slice-done
  50.4 0.0 slice-done.1
  50.4 0.0 slice-start.3
  50.4 0.0 copy-start
  50.4 0.0 copy-start.1
  50.4 2.9 %moment.1 = (f32[1024,2304]{1,0:T(8,128)S(1)}, bf16[1024,2304]{1,0:T(8,128)(2,1)}) custom-call(f32[1024,2304]{1,0:T(8,128)S(1)} %get-tuple-element.43.grad_ref, f32[1024,128]{1,0:T(8,128)S(1)} %get-tuple-element.44.count_ref, bf16[1024,2304]{1,0:T(8,128)(2,1)S(1)} %bitcast.6), custom_call_target="tpu_custom_call" | custom-call | flops 1000000000 | bytes 4718592 | tf_op jit(solution)/shard_map/moment/pallas_call | solution.py:279
  53.3 0.0 collective-permute-done.15.other_ref
  53.3 0.0 slice-done.2
  53.3 0.0 slice-done.3
  53.3 0.0 copy-done
  53.4 0.0 copy-done.1
  53.4 3.7 %weights.1 = (bf16[1024,2304]{1,0:T(8,128)(2,1)}, f32[8,128]{1,0:T(8,128)}) custom-call(f32[1024,2304]{1,0:T(8,128)S(1)} %get-tuple-element.45.first_ref, bf16[1024,2304]{1,0:T(8,128)(2,1)S(1)} %bitcast.8, f32[8,128]{1,0:T(8,128)S(1)} %get-tuple-element.46.mine_ref, f32[8,128]{1,0:T(8,128)S(1)} %collective-permute-done.15.other_ref, ...), custom_call_target="tpu_custom_call" | custom-call | tf_op jit(solution)/shard_map/weights/pallas_call | solution.py:289
  (2 shorter events, 0.0 us)
Async XLA Ops:
  0.6 49.8 %slice-start = ((s8[4718592]{0:T(1024)(128)(4,1)}), s8[524288]{0:T(1024)(128)(4,1)S(1)}, s32[]{:S(2)}) async-start(s8[4718592]{0:T(1024)(128)(4,1)} %bitcast.5), calls=%async_computation | async-start | bytes 1048576
  0.6 49.8 %slice-start.1 = ((s8[4718592]{0:T(1024)(128)(4,1)}), s8[4194304]{0:T(1024)(128)(4,1)S(1)}, s32[]{:S(2)}) async-start(s8[4718592]{0:T(1024)(128)(4,1)} %bitcast.5), calls=%async_computation.1 | async-start | bytes 8388608
  6.7 9.8 %collective-permute-start = (bf16[296,128]{1,0:T(8,128)(2,1)S(1)}, bf16[296,128]{1,0:T(8,128)(2,1)S(1)}, u32[]{:S(2)}, u32[]{:S(2)}) collective-permute-start(bf16[296,128]{1,0:T(8,128)(2,1)S(1)} %get-tuple-element.28), channel_id=1, source_target_pairs={{0,2},{2,0},{4,6},{6,4},{8,10},{10,8},{12,14},{14,12},{16,18},{18,... | collective-permute-start | bytes 227336 | tf_op jit(solution)/shard_map/ppermute | solution.py:264
  8.8 9.7 %collective-permute-start.1 = (bf16[296,128]{1,0:T(8,128)(2,1)S(1)}, bf16[296,128]{1,0:T(8,128)(2,1)S(1)}, u32[]{:S(2)}, u32[]{:S(2)}) collective-permute-start(bf16[296,128]{1,0:T(8,128)(2,1)S(1)} %get-tuple-element.29), channel_id=1, source_target_pairs={{0,4},{2,6},{4,0},{6,2},{8,12},{10,14},{12,8},{14,10},{16,20},{18,... | collective-permute-start | bytes 227336 | tf_op jit(solution)/shard_map/ppermute | solution.py:264
  10.1 10.6 %collective-permute-start.10 = (bf16[296,128]{1,0:T(8,128)(2,1)S(1)}, bf16[296,128]{1,0:T(8,128)(2,1)S(1)}, u32[]{:S(2)}, u32[]{:S(2)}) collective-permute-start(bf16[296,128]{1,0:T(8,128)(2,1)S(1)} %get-tuple-element.38), channel_id=1, source_target_pairs={{0,22},{2,20},{4,18},{6,16},{8,30},{10,28},{12,26},{14,24},{16,6},... | collective-permute-start | bytes 227336 | tf_op jit(solution)/shard_map/ppermute | solution.py:264
  12.3 10.5 %collective-permute-start.11 = (bf16[296,128]{1,0:T(8,128)(2,1)S(1)}, bf16[296,128]{1,0:T(8,128)(2,1)S(1)}, u32[]{:S(2)}, u32[]{:S(2)}) collective-permute-start(bf16[296,128]{1,0:T(8,128)(2,1)S(1)} %get-tuple-element.39), channel_id=1, source_target_pairs={{0,24},{2,26},{4,28},{6,30},{8,16},{10,18},{12,20},{14,22},{16,8},... | collective-permute-start | bytes 227336 | tf_op jit(solution)/shard_map/ppermute | solution.py:264
  13.4 9.7 %collective-permute-start.12 = (bf16[296,128]{1,0:T(8,128)(2,1)S(1)}, bf16[296,128]{1,0:T(8,128)(2,1)S(1)}, u32[]{:S(2)}, u32[]{:S(2)}) collective-permute-start(bf16[296,128]{1,0:T(8,128)(2,1)S(1)} %get-tuple-element.40), channel_id=1, source_target_pairs={{0,26},{2,24},{4,30},{6,28},{8,18},{10,16},{12,22},{14,20},{16,10}... | collective-permute-start | bytes 227336 | tf_op jit(solution)/shard_map/ppermute | solution.py:264
  16.5 11.0 %collective-permute-start.13 = (bf16[296,128]{1,0:T(8,128)(2,1)S(1)}, bf16[296,128]{1,0:T(8,128)(2,1)S(1)}, u32[]{:S(2)}, u32[]{:S(2)}) collective-permute-start(bf16[296,128]{1,0:T(8,128)(2,1)S(1)} %get-tuple-element.41), channel_id=1, source_target_pairs={{0,28},{2,30},{4,24},{6,26},{8,20},{10,22},{12,16},{14,18},{16,12}... | collective-permute-start | bytes 227336 | tf_op jit(solution)/shard_map/ppermute | solution.py:264
  18.5 10.9 %collective-permute-start.14 = (bf16[296,128]{1,0:T(8,128)(2,1)S(1)}, bf16[296,128]{1,0:T(8,128)(2,1)S(1)}, u32[]{:S(2)}, u32[]{:S(2)}) collective-permute-start(bf16[296,128]{1,0:T(8,128)(2,1)S(1)} %get-tuple-element.42), channel_id=1, source_target_pairs={{0,30},{2,28},{4,26},{6,24},{8,22},{10,20},{12,18},{14,16},{16,14}... | collective-permute-start | bytes 227336 | tf_op jit(solution)/shard_map/ppermute | solution.py:264
  20.6 11.5 %collective-permute-start.2 = (bf16[296,128]{1,0:T(8,128)(2,1)S(1)}, bf16[296,128]{1,0:T(8,128)(2,1)S(1)}, u32[]{:S(2)}, u32[]{:S(2)}) collective-permute-start(bf16[296,128]{1,0:T(8,128)(2,1)S(1)} %get-tuple-element.30), channel_id=1, source_target_pairs={{0,6},{2,4},{4,2},{6,0},{8,14},{10,12},{12,10},{14,8},{16,22},{18,... | collective-permute-start | bytes 227336 | tf_op jit(solution)/shard_map/ppermute | solution.py:264
  22.8 11.7 %collective-permute-start.3 = (bf16[296,128]{1,0:T(8,128)(2,1)S(1)}, bf16[296,128]{1,0:T(8,128)(2,1)S(1)}, u32[]{:S(2)}, u32[]{:S(2)}) collective-permute-start(bf16[296,128]{1,0:T(8,128)(2,1)S(1)} %get-tuple-element.31), channel_id=1, source_target_pairs={{0,8},{2,10},{4,12},{6,14},{8,0},{10,2},{12,4},{14,6},{16,24},{18,... | collective-permute-start | bytes 227336 | tf_op jit(solution)/shard_map/ppermute | solution.py:264
  23.1 12.6 %collective-permute-start.4 = (bf16[296,128]{1,0:T(8,128)(2,1)S(1)}, bf16[296,128]{1,0:T(8,128)(2,1)S(1)}, u32[]{:S(2)}, u32[]{:S(2)}) collective-permute-start(bf16[296,128]{1,0:T(8,128)(2,1)S(1)} %get-tuple-element.32), channel_id=1, source_target_pairs={{0,10},{2,8},{4,14},{6,12},{8,2},{10,0},{12,6},{14,4},{16,26},{18,... | collective-permute-start | bytes 227336 | tf_op jit(solution)/shard_map/ppermute | solution.py:264
  27.5 9.3 %collective-permute-start.5 = (bf16[296,128]{1,0:T(8,128)(2,1)S(1)}, bf16[296,128]{1,0:T(8,128)(2,1)S(1)}, u32[]{:S(2)}, u32[]{:S(2)}) collective-permute-start(bf16[296,128]{1,0:T(8,128)(2,1)S(1)} %get-tuple-element.33), channel_id=1, source_target_pairs={{0,12},{2,14},{4,8},{6,10},{8,4},{10,6},{12,0},{14,2},{16,28},{18,... | collective-permute-start | bytes 227336 | tf_op jit(solution)/shard_map/ppermute | solution.py:264
  29.4 7.4 %collective-permute-start.6 = (bf16[296,128]{1,0:T(8,128)(2,1)S(1)}, bf16[296,128]{1,0:T(8,128)(2,1)S(1)}, u32[]{:S(2)}, u32[]{:S(2)}) collective-permute-start(bf16[296,128]{1,0:T(8,128)(2,1)S(1)} %get-tuple-element.34), channel_id=1, source_target_pairs={{0,14},{2,12},{4,10},{6,8},{8,6},{10,4},{12,2},{14,0},{16,30},{18,... | collective-permute-start | bytes 227336 | tf_op jit(solution)/shard_map/ppermute | solution.py:264
  32.1 4.7 %collective-permute-start.7 = (bf16[296,128]{1,0:T(8,128)(2,1)S(1)}, bf16[296,128]{1,0:T(8,128)(2,1)S(1)}, u32[]{:S(2)}, u32[]{:S(2)}) collective-permute-start(bf16[296,128]{1,0:T(8,128)(2,1)S(1)} %get-tuple-element.35), channel_id=1, source_target_pairs={{0,16},{2,18},{4,20},{6,22},{8,24},{10,26},{12,28},{14,30},{16,0},... | collective-permute-start | bytes 227336 | tf_op jit(solution)/shard_map/ppermute | solution.py:264
  34.5 10.3 %collective-permute-start.8 = (bf16[296,128]{1,0:T(8,128)(2,1)S(1)}, bf16[296,128]{1,0:T(8,128)(2,1)S(1)}, u32[]{:S(2)}, u32[]{:S(2)}) collective-permute-start(bf16[296,128]{1,0:T(8,128)(2,1)S(1)} %get-tuple-element.36), channel_id=1, source_target_pairs={{0,18},{2,16},{4,22},{6,20},{8,26},{10,24},{12,30},{14,28},{16,2},... | collective-permute-start | bytes 227336 | tf_op jit(solution)/shard_map/ppermute | solution.py:264
  35.7 10.2 %collective-permute-start.9 = (bf16[296,128]{1,0:T(8,128)(2,1)S(1)}, bf16[296,128]{1,0:T(8,128)(2,1)S(1)}, u32[]{:S(2)}, u32[]{:S(2)}) collective-permute-start(bf16[296,128]{1,0:T(8,128)(2,1)S(1)} %get-tuple-element.37), channel_id=1, source_target_pairs={{0,20},{2,22},{4,16},{6,18},{8,28},{10,30},{12,24},{14,26},{16,4},... | collective-permute-start | bytes 227336 | tf_op jit(solution)/shard_map/ppermute | solution.py:264
  45.9 7.4 %slice-start.2 = ((s8[4718592]{0:T(1024)(128)(4,1)}), s8[4194304]{0:T(1024)(128)(4,1)S(1)}, s32[]{:S(2)}) async-start(s8[4718592]{0:T(1024)(128)(4,1)} %bitcast.7), calls=%async_computation.2 | async-start | bytes 8388608
  49.1 4.2 %collective-permute-start.15 = (f32[8,128]{1,0:T(8,128)S(1)}, f32[8,128]{1,0:T(8,128)S(1)}, u32[]{:S(2)}, u32[]{:S(2)}) collective-permute-start(f32[8,128]{1,0:T(8,128)S(1)} %get-tuple-element.46.mine_ref), channel_id=1, source_target_pairs={{0,1},{1,0},{2,3},{3,2},{4,5},{5,4},{6,7},{7,6},{8,9},{9,8},{10,11... | collective-permute-start | bytes 12296 | tf_op jit(solution)/shard_map/ppermute | solution.py:278
  50.4 2.9 %slice-start.3 = ((s8[4718592]{0:T(1024)(128)(4,1)}), s8[524288]{0:T(1024)(128)(4,1)S(1)}, s32[]{:S(2)}) async-start(s8[4718592]{0:T(1024)(128)(4,1)} %bitcast.7), calls=%async_computation.3 | async-start | bytes 1048576
  50.4 2.9 %copy-start = (f32[1024]{0:T(1024)S(1)}, f32[1024]{0:T(1024)}, u32[]{:S(2)}) copy-start(f32[1024]{0:T(1024)} %param.14) | copy-start | bytes 12292
  50.4 2.9 %copy-start.1 = (s32[1024]{0:T(1024)S(1)}, s32[1024]{0:T(1024)}, u32[]{:S(2)}) copy-start(s32[1024]{0:T(1024)} %param.15) | copy-start | bytes 12292

commit v2 on v1

--- a/solution.py
+++ b/solution.py
@@ -95,10 +95,49 @@
                 ]
 
 
-def grad_kernel(owners, cap, *refs):
+def eye():
+    return iota((LANES, LANES), 0) == iota((LANES, LANES), 1)
+
+
+def to_column(line):
+    return jnp.sum(jnp.where(eye(), line, 0.0), axis=1, keepdims=True)
+
+
+def to_line(column):
+    return jnp.sum(jnp.where(eye(), column, 0.0), axis=0, keepdims=True)
+
+
+def fetch_kernel(
+    weights_far, moment_far, scale_ref, steps_ref, weights_ref, moment_ref, rate_ref, fix_ref, row_ref, sems
+):
+    copies = [
+        pltpu.make_async_copy(moment_far, moment_ref, sems.at[0]),
+        pltpu.make_async_copy(weights_far, weights_ref, sems.at[1]),
+    ]
+    for copy in copies:
+        copy.start()
+    steps = (steps_ref[...] + 1).astype(F32)
+    rate = 0.01 / (1.0 - jnp.exp(steps * jnp.log(jnp.float32(0.9))))
+    fix = 1.0 / (1.0 - jnp.exp(steps * jnp.log(jnp.float32(0.95))))
+    for i in range(steps.shape[0]):
+        part = slice(i * LANES, (i + 1) * LANES)
+        for line, ref in ((rate, rate_ref), (fix, fix_ref), (scale_ref, row_ref)):
+            ref[part, :] = jnp.broadcast_to(to_column(line[i : i + 1, :]), (LANES, LANES))
+    for copy in copies:
+        copy.wait()
+
+
+def gather_columns(blocks, cap, c, step):
+    parts = []
+    for t in range(step // LANES):
+        at = (c // LANES + t) * cap
+        parts.append(jnp.concatenate([b[at : at + cap, :] for b in blocks], axis=0))
+    return jnp.concatenate(parts, axis=1) if len(parts) > 1 else parts[0]
+
+
+def square_kernel(owners, cap, half, *refs):
     blocks = refs[:owners]
-    grad_ref, squares_ref, hits_ref, count_ref, place, acc = refs[owners:]
-    rows, half = grad_ref.shape
+    squares_ref, names_ref, same = refs[owners:]
     slots = owners * cap
     groups = slots // LANES
     step = col_step(half)
@@ -106,96 +145,91 @@
     names = blocks[0][base:, :].astype(F32)
     for d in range(1, owners):
         names = names + blocks[d][base:, :].astype(F32)
-    names = names.astype(I32)
+    row = (names[0:groups, :] - 1.0) * LANES + names[groups : 2 * groups, :]
+    names_ref[...] = row.astype(I32)
     for g in range(groups):
-        row = (names[g : g + 1, :] - 1) * LANES + names[groups + g : groups + g + 1, :]
-        hit = row == iota((rows, LANES), 0)
+        column = to_column(row[g : g + 1, :])
+        for h in range(groups):
+            hit = column == row[h : h + 1, :]
+            same[g * LANES : (g + 1) * LANES, h * LANES : (h + 1) * LANES] = jnp.where(
+                hit, 1.0, 0.0
+            ).astype(BF16)
+    total = None
+    for c in range(0, half, step):
+        got = jnp.dot(
+            same[...], gather_columns(blocks, cap, c, step), preferred_element_type=F32
+        )
+        for t in range(step // LANES):
+            x = got[:, t * LANES : (t + 1) * LANES]
+            total = x * x if total is None else total + x * x
+    for g in range(groups):
+        column = jnp.sum(total[g * LANES : (g + 1) * LANES, :], axis=1, keepdims=True)
+        squares_ref[g : g + 1, :] = to_line(column)
+
+
+def moment_kernel(owners, cap, *refs):
+    blocks, names_ref, moment_ref = refs[:owners], refs[owners], refs[owners + 1]
+    first_ref, new_ref, place, keep, staged, sems = refs[owners + 2 :]
+    rows, half = moment_ref.shape
+    slots = owners * cap
+    step = col_step(half)
+    for g in range(slots // LANES):
+        hit = names_ref[g : g + 1, :] == iota((rows, LANES), 0)
         place[:, g * LANES : (g + 1) * LANES] = jnp.where(hit, 1.0, 0.0).astype(BF16)
-    count_ref[...] = jnp.dot(
-        place[...], jnp.ones((slots, LANES), BF16), preferred_element_type=F32
-    )
+    count = jnp.dot(place[...], jnp.ones((slots, LANES), BF16), preferred_element_type=F32)
+    keep[...] = jnp.where(count > 0.0, 0.9, 1.0)
+    copies = []
+    block = min(rows, 2 * LANES)
     for c in range(0, half, step):
-        parts = []
-        for t in range(step // LANES):
-            at = (c // LANES + t) * cap
-            parts.append(jnp.concatenate([b[at : at + cap, :] for b in blocks], axis=0))
-        got = jnp.concatenate(parts, axis=1) if len(parts) > 1 else parts[0]
-        grad_ref[:, c : c + step] = jnp.dot(place[...], got, preferred_element_type=F32)
-        for r in range(0, rows, LANES):
-            total = acc[r : r + LANES, :] if c else None
+        got = gather_columns(blocks, cap, c, step)
+        for r in range(0, rows, block):
+            part = slice(r, r + block)
+            grad = jnp.dot(place[part, :], got, preferred_element_type=F32)
             for t in range(step // LANES):
-                x = grad_ref[r : r + LANES, c + t * LANES : c + (t + 1) * LANES]
-                total = x * x if total is None else total + x * x
-            acc[r : r + LANES, :] = total
-    one = jnp.ones((8, LANES), F32)
-    lanes = (((1,), (1,)), ((), ()))
-    for r in range(rows // LANES):
-        part = slice(r * LANES, (r + 1) * LANES)
-        squares_ref[r : r + 1, :] = lax.dot_general(
-            one, acc[part, :], lanes, precision=lax.Precision.HIGHEST, preferred_element_type=F32
-        )[0:1, :]
-        hits_ref[r : r + 1, :] = lax.dot_general(
-            one, count_ref[part, :], lanes, precision=lax.Precision.HIGHEST, preferred_element_type=F32
-        )[0:1, :]
-
-
-def moment_kernel(grad_ref, count_ref, moment_ref, first_ref, new_ref, staged, sems):
-    rows, half = grad_ref.shape
-    strip = 16
-
-    def copy(i):
-        part = pl.ds(pl.multiple_of(i * LANES, LANES), LANES)
-        return pltpu.make_async_copy(staged.at[part, :], new_ref.at[part, :], sems.at[i])
-
-    @pl.loop(0, rows // LANES)
-    def _(i):
-        @pl.loop(0, LANES // strip)
-        def _(j):
-            part = pl.ds(pl.multiple_of(i * LANES + j * strip, strip), strip)
-            keep = jnp.where(count_ref[part, :] > 0.0, 0.9, 1.0)
-            for c in range(0, half, LANES):
-                old = moment_ref[part, c : c + LANES].astype(F32)
-                first = keep * old + 0.1 * grad_ref[part, c : c + LANES]
-                first_ref[part, c : c + LANES] = first
-                staged[part, c : c + LANES] = first.astype(BF16)
-
-        copy(i).start()
-
-    @pl.loop(0, rows // LANES)
-    def _(i):
-        copy(i).wait()
+                at = slice(c + t * LANES, c + (t + 1) * LANES)
+                first = keep[part, :] * moment_ref[part, at].astype(F32)
+                first = first + 0.1 * grad[:, t * LANES : (t + 1) * LANES]
+                first_ref[part, at] = first
+                staged[part, at] = first.astype(BF16)
+        at = pl.ds(c, step)
+        copy = pltpu.make_async_copy(staged.at[:, at], new_ref.at[:, at], sems.at[c // step])
+        copy.start()
+        copies.append(copy)
+    for copy in copies:
+        copy.wait()
 
 
 def weights_kernel(
-    width, first_ref, weights_ref, mine_ref, other_ref, hits_ref, scale_ref, steps_ref,
+    width, first_ref, weights_ref, mine_ref, other_ref, names_ref, rate_ref, fix_ref, row_ref,
     new_ref, new_scale_ref, staged, rates, sems,
 ):
     rows, half = first_ref.shape
-    square = (mine_ref[...] + other_ref[...]) / width
-    touched = hits_ref[...] > 0.5
-    scale = scale_ref[...]
-    second = jnp.where(touched, 0.95 * scale + 0.05 * square, scale)
-    new_scale_ref[...] = second
-    steps = (steps_ref[...] + 1).astype(F32)
-    fix_first = 1.0 - jnp.exp(steps * jnp.log(jnp.float32(0.9)))
-    fix_second = 1.0 - jnp.exp(steps * jnp.log(jnp.float32(0.95)))
-    denom = jnp.sqrt(second / fix_second) + 1e-08
-    rate = jnp.where(touched, 0.01 / (fix_first * denom), -1.0)
-    eye = iota((LANES, LANES), 0) == iota((LANES, LANES), 1)
+    groups = names_ref.shape[0]
+    square = mine_ref[...] + other_ref[...]
+    names = names_ref[...]
+
+    def scalars(i):
+        part = slice(i * LANES, (i + 1) * LANES)
+        ids = iota((LANES, LANES), 0) + i * LANES
+        most = jnp.full((LANES, LANES), -1.0, F32)
+        for g in range(groups):
+            hit = names[g : g + 1, :] == ids
+            most = jnp.maximum(most, jnp.where(hit, square[g : g + 1, :], -1.0))
+        most = jnp.broadcast_to(jnp.max(most, axis=1, keepdims=True), (LANES, LANES))
+        touched = most >= 0.0
+        scale = row_ref[part, :]
+        second = jnp.where(touched, 0.95 * scale + 0.05 * (most / width), scale)
+        new_scale_ref[i : i + 1, :] = to_line(second)
+        denom = jnp.sqrt(second * fix_ref[part, :]) + 1e-08
+        rates[part, :] = jnp.where(touched, rate_ref[part, :] / denom, -1.0)
+
+    copies = []
+    strip = 16
     for i in range(rows // LANES):
-        column = jnp.sum(jnp.where(eye, rate[i : i + 1, :], 0.0), axis=1, keepdims=True)
-        rates[i * LANES : (i + 1) * LANES, :] = jnp.broadcast_to(column, (LANES, LANES))
-    strip = 16
-
-    def copy(i):
-        part = pl.ds(pl.multiple_of(i * LANES, LANES), LANES)
-        return pltpu.make_async_copy(staged.at[part, :], new_ref.at[part, :], sems.at[i])
-
-    @pl.loop(0, rows // LANES)
-    def _(i):
-        @pl.loop(0, LANES // strip)
-        def _(j):
-            part = pl.ds(pl.multiple_of(i * LANES + j * strip, strip), strip)
+        scalars(i)
+    for i in range(rows // LANES):
+        for r in range(i * LANES, (i + 1) * LANES, strip):
+            part = slice(r, r + strip)
             rate = rates[part, :]
             keep = jnp.where(rate < 0.0, 1.0, 0.999)
             rate = jnp.maximum(rate, 0.0)
@@ -203,12 +237,12 @@
                 old = weights_ref[part, c : c + LANES].astype(F32)
                 new = keep * old - rate * first_ref[part, c : c + LANES]
                 staged[part, c : c + LANES] = new.astype(BF16)
-
-        copy(i).start()
-
-    @pl.loop(0, rows // LANES)
-    def _(i):
-        copy(i).wait()
+        part = pl.ds(i * LANES, LANES)
+        copy = pltpu.make_async_copy(staged.at[part, :], new_ref.at[part, :], sems.at[i])
+        copy.start()
+        copies.append(copy)
+    for copy in copies:
+        copy.wait()
 
 
 def near(x):
@@ -263,40 +297,66 @@
     for d in range(1, owners):
         received[d] = lax.ppermute(outgoing[d], "vocab", [(s, s ^ d) for s in range(owners)])
     lined = jax.ShapeDtypeStruct((rows // LANES, LANES), F32)
-    grad, squares, hits, count = pl.pallas_call(
-        functools.partial(grad_kernel, owners, cap),
-        out_shape=[pltpu.VMEM((rows, half), F32), lined, lined, pltpu.VMEM((rows, LANES), F32)],
+    wide = pltpu.VMEM((rows, LANES), F32)
+    kept = pltpu.VMEM((rows, half), BF16)
+    weights_near, moment_near, rate, fix, scale = pl.pallas_call(
+        fetch_kernel,
+        out_shape=[kept, kept, wide, wide, wide],
+        in_specs=[ANY, ANY, VMEM, VMEM],
+        out_specs=[VMEM] * 5,
+        scratch_shapes=[pltpu.SemaphoreType.DMA((2,))],
+        compiler_params=params(4),
+        name="fetch",
+    )(
+        far(weights), far(moment), row_scale.reshape(rows // LANES, LANES),
+        row_steps.reshape(rows // LANES, LANES),
+    )
+    blocks = [received[d] for d in range(owners)]
+    sloted = (slots // LANES, LANES)
+    squares, names = pl.pallas_call(
+        functools.partial(square_kernel, owners, cap, half),
+        out_shape=[jax.ShapeDtypeStruct(sloted, F32), jax.ShapeDtypeStruct(sloted, I32)],
         in_specs=[VMEM] * owners,
-        out_specs=[VMEM] * 4,
-        scratch_shapes=[pltpu.VMEM((rows, slots), BF16), pltpu.VMEM((rows, LANES), F32)],
-        compiler_params=params(12),
+        out_specs=[VMEM] * 2,
+        scratch_shapes=[pltpu.VMEM((slots, slots), BF16)],
+        compiler_params=params(10),
         cost_estimate=pl.CostEstimate(
-            flops=2 * slots * rows * half, bytes_accessed=slots * half * 2, transcendentals=0
+            flops=2 * slots * slots * half, bytes_accessed=slots * half * 2, transcendentals=0
         ),
-        name="grad",
-    )(*[received[d] for d in range(owners)])
+        name="square",
+    )(*blocks)
     other = lax.ppermute(squares, "width", [(s, halves - 1 - s) for s in range(halves)])
     first, new_moment = pl.pallas_call(
-        moment_kernel,
+        functools.partial(moment_kernel, owners, cap),
         out_shape=[pltpu.VMEM((rows, half), F32), jax.ShapeDtypeStruct((rows, half), BF16)],
-        in_specs=[VMEM] * 3,
+        in_specs=[VMEM] * (owners + 2),
         out_specs=[VMEM, ANY],
-        scratch_shapes=[pltpu.VMEM((rows, half), BF16), pltpu.SemaphoreType.DMA((rows // LANES,))],
+        scratch_shapes=[
+            pltpu.VMEM((rows, slots), BF16),
+            pltpu.VMEM((rows, LANES), F32),
+            pltpu.VMEM((rows, half), BF16),
+            pltpu.SemaphoreType.DMA((half // step,)),
+        ],
         compiler_params=params(16),
-        cost_estimate=pl.CostEstimate(flops=10**9, bytes_accessed=2 * rows * half, transcendentals=0),
+        cost_estimate=pl.CostEstimate(
+            flops=2 * slots * rows * half, bytes_accessed=2 * rows * half, transcendentals=0
+        ),
         name="moment",
-    )(near(grad), near(count), near(moment))
+    )(*blocks, names, near(moment_near))
     new_weights, new_scale = pl.pallas_call(
         functools.partial(weights_kernel, halves * half),
         out_shape=[jax.ShapeDtypeStruct((rows, half), BF16), lined],
-        in_specs=[VMEM] * 7,
+        in_specs=[VMEM] * 8,
         out_specs=[ANY, VMEM],
-        scratch_shapes=[pltpu.VMEM((rows, half), BF16), pltpu.VMEM((rows, LANES), F32), pltpu.SemaphoreType.DMA((rows // LANES,))],
-        compiler_params=params(16),
+        scratch_shapes=[
+            pltpu.VMEM((rows, half), BF16),
+            pltpu.VMEM((rows, LANES), F32),
+            pltpu.SemaphoreType.DMA((rows // LANES,)),
+        ],
+        compiler_params=params(10),
         name="weights",
     )(
-        near(first), near(weights), squares, other, hits,
-        row_scale.reshape(rows // LANES, LANES), row_steps.reshape(rows // LANES, LANES),
+        near(first), near(weights_near), squares, other, names, near(rate), near(fix), near(scale),
     )
     return new_weights, new_moment, new_scale.reshape(rows)
 

time: 57.3 us -> 54.7 us (0.955)
  the two profiles are of different devices: /device:TPU:1 before, /device:TPU:0 now
where the time goes in v2:
time: 54.7 us; the launch traced here: 54.5 us
  starting transfers between devices  32.4 us (59%)
  Pallas kernels  17.1 us (31%)
  waiting for transfers between devices  4.26 us (8%)
  between operations  0.73 us (1%)
    ppermute x15, starting transfers between devices, shards(): lax.ppermute(outgoing[d], 'vocab', [(s, s ^ d) for s in range(owners)])  32.3 us
    pallas_call x1, Pallas kernels, shards(): pl.pallas_call(functools.partial(send_kernel, owners, cap), out_shape=[bl...  5.93 us
    ppermute x15, waiting for transfers between devices, shards(): lax.ppermute(outgoing[d], 'vocab', [(s, s ^ d) for s in range(owners)])  4.26 us
    pallas_call x1, Pallas kernels, shards(): pl.pallas_call(fetch_kernel, out_shape=[kept, kept, wide, wide, wide], in...  3.79 us
    pallas_call x1, Pallas kernels, shards(): pl.pallas_call(functools.partial(weights_kernel, halves * half), out_shap...  3.58 us
    pallas_call x1, Pallas kernels, shards(): pl.pallas_call(functools.partial(moment_kernel, owners, cap), out_shape=[...  3.17 us
  transfers between devices with their start and end apart: 16, of which 3 were waited for; matrix products, arithmetic and copies ran while one was open for 0% of the time, Pallas kernels for 13%

profile of v2, /device:TPU:0, one launch (start us, length us, event | category | flops | bytes accessed | tf_op | source)
XLA Modules:
  0.0 54.5 jit_solution(14157796471090129129)
XLA Ops:
  0.6 0.0 copy-start
  0.6 0.0 copy-start.1
  0.7 5.9 %send.1 = (bf16[296,128]{1,0:T(8,128)(2,1)S(1)}, bf16[296,128]{1,0:T(8,128)(2,1)S(1)}, bf16[296,128]{1,0:T(8,128)(2,1)S(1)}, bf16[296,128]{1,0:T(8,128)(2,1)S(1)...) custom-call(s32[1]{0:T(128)} %bitcast.me_ref, ...), custom_call_target="tpu_custom_call" | custom-call | flops 1207959552 | bytes 4718592 | tf_op jit(solution)/shard_map/send/pallas_call | solution.py:273
  6.6 3.0 %collective-permute-start = (bf16[296,128]{1,0:T(8,128)(2,1)S(1)}, bf16[296,128]{1,0:T(8,128)(2,1)S(1)}, u32[]{:S(2)}, u32[]{:S(2)}) collective-permute-start(bf16[296,128]{1,0:T(8,128)(2,1)S(1)} %get-tuple-element.31), channel_id=1, source_target_pairs={{0,2},{2,0},{4,6},{6,4},{8,10},{10,8},{12,14},{14,12},{16,18},{18,... | collective-permute-start | bytes 227336 | tf_op jit(solution)/shard_map/ppermute | solution.py:298
  9.6 1.5 %collective-permute-start.1 = (bf16[296,128]{1,0:T(8,128)(2,1)S(1)}, bf16[296,128]{1,0:T(8,128)(2,1)S(1)}, u32[]{:S(2)}, u32[]{:S(2)}) collective-permute-start(bf16[296,128]{1,0:T(8,128)(2,1)S(1)} %get-tuple-element.32), channel_id=1, source_target_pairs={{0,4},{2,6},{4,0},{6,2},{8,12},{10,14},{12,8},{14,10},{16,20},{18,... | collective-permute-start | bytes 227336 | tf_op jit(solution)/shard_map/ppermute | solution.py:298
  11.1 2.5 %collective-permute-start.10 = (bf16[296,128]{1,0:T(8,128)(2,1)S(1)}, bf16[296,128]{1,0:T(8,128)(2,1)S(1)}, u32[]{:S(2)}, u32[]{:S(2)}) collective-permute-start(bf16[296,128]{1,0:T(8,128)(2,1)S(1)} %get-tuple-element.41), channel_id=1, source_target_pairs={{0,22},{2,20},{4,18},{6,16},{8,30},{10,28},{12,26},{14,24},{16,6},... | collective-permute-start | bytes 227336 | tf_op jit(solution)/shard_map/ppermute | solution.py:298
  13.6 1.3 %collective-permute-start.11 = (bf16[296,128]{1,0:T(8,128)(2,1)S(1)}, bf16[296,128]{1,0:T(8,128)(2,1)S(1)}, u32[]{:S(2)}, u32[]{:S(2)}) collective-permute-start(bf16[296,128]{1,0:T(8,128)(2,1)S(1)} %get-tuple-element.42), channel_id=1, source_target_pairs={{0,24},{2,26},{4,28},{6,30},{8,16},{10,18},{12,20},{14,22},{16,8},... | collective-permute-start | bytes 227336 | tf_op jit(solution)/shard_map/ppermute | solution.py:298
  15.0 3.4 %collective-permute-start.12 = (bf16[296,128]{1,0:T(8,128)(2,1)S(1)}, bf16[296,128]{1,0:T(8,128)(2,1)S(1)}, u32[]{:S(2)}, u32[]{:S(2)}) collective-permute-start(bf16[296,128]{1,0:T(8,128)(2,1)S(1)} %get-tuple-element.43), channel_id=1, source_target_pairs={{0,26},{2,24},{4,30},{6,28},{8,18},{10,16},{12,22},{14,20},{16,10}... | collective-permute-start | bytes 227336 | tf_op jit(solution)/shard_map/ppermute | solution.py:298
  18.4 0.0 collective-permute-done.refs_1_
  18.4 2.3 %collective-permute-start.13 = (bf16[296,128]{1,0:T(8,128)(2,1)S(1)}, bf16[296,128]{1,0:T(8,128)(2,1)S(1)}, u32[]{:S(2)}, u32[]{:S(2)}) collective-permute-start(bf16[296,128]{1,0:T(8,128)(2,1)S(1)} %get-tuple-element.44), channel_id=1, source_target_pairs={{0,28},{2,30},{4,24},{6,26},{8,20},{10,22},{12,16},{14,18},{16,12}... | collective-permute-start | bytes 227336 | tf_op jit(solution)/shard_map/ppermute | solution.py:298
  20.7 0.0 collective-permute-done.1.refs_2_
  20.7 2.4 %collective-permute-start.14 = (bf16[296,128]{1,0:T(8,128)(2,1)S(1)}, bf16[296,128]{1,0:T(8,128)(2,1)S(1)}, u32[]{:S(2)}, u32[]{:S(2)}) collective-permute-start(bf16[296,128]{1,0:T(8,128)(2,1)S(1)} %get-tuple-element.45), channel_id=1, source_target_pairs={{0,30},{2,28},{4,26},{6,24},{8,22},{10,20},{12,18},{14,16},{16,14}... | collective-permute-start | bytes 227336 | tf_op jit(solution)/shard_map/ppermute | solution.py:298
  23.1 0.0 collective-permute-done.10.refs_11_
  23.1 2.4 %collective-permute-start.2 = (bf16[296,128]{1,0:T(8,128)(2,1)S(1)}, bf16[296,128]{1,0:T(8,128)(2,1)S(1)}, u32[]{:S(2)}, u32[]{:S(2)}) collective-permute-start(bf16[296,128]{1,0:T(8,128)(2,1)S(1)} %get-tuple-element.33), channel_id=1, source_target_pairs={{0,6},{2,4},{4,2},{6,0},{8,14},{10,12},{12,10},{14,8},{16,22},{18,... | collective-permute-start | bytes 227336 | tf_op jit(solution)/shard_map/ppermute | solution.py:298
  25.6 0.0 collective-permute-done.11.refs_12_
  25.6 0.0 collective-permute-start.3
  25.6 0.0 collective-permute-done.12.refs_13_
  25.6 3.2 %collective-permute-start.4 = (bf16[296,128]{1,0:T(8,128)(2,1)S(1)}, bf16[296,128]{1,0:T(8,128)(2,1)S(1)}, u32[]{:S(2)}, u32[]{:S(2)}) collective-permute-start(bf16[296,128]{1,0:T(8,128)(2,1)S(1)} %get-tuple-element.35), channel_id=1, source_target_pairs={{0,10},{2,8},{4,14},{6,12},{8,2},{10,0},{12,6},{14,4},{16,26},{18,... | collective-permute-start | bytes 227336 | tf_op jit(solution)/shard_map/ppermute | solution.py:298
  28.8 0.0 collective-permute-done.13.refs_14_
  28.8 1.6 %collective-permute-start.5 = (bf16[296,128]{1,0:T(8,128)(2,1)S(1)}, bf16[296,128]{1,0:T(8,128)(2,1)S(1)}, u32[]{:S(2)}, u32[]{:S(2)}) collective-permute-start(bf16[296,128]{1,0:T(8,128)(2,1)S(1)} %get-tuple-element.36), channel_id=1, source_target_pairs={{0,12},{2,14},{4,8},{6,10},{8,4},{10,6},{12,0},{14,2},{16,28},{18,... | collective-permute-start | bytes 227336 | tf_op jit(solution)/shard_map/ppermute | solution.py:298
  30.4 0.0 collective-permute-done.14.refs_15_
  30.4 2.8 %collective-permute-start.6 = (bf16[296,128]{1,0:T(8,128)(2,1)S(1)}, bf16[296,128]{1,0:T(8,128)(2,1)S(1)}, u32[]{:S(2)}, u32[]{:S(2)}) collective-permute-start(bf16[296,128]{1,0:T(8,128)(2,1)S(1)} %get-tuple-element.37), channel_id=1, source_target_pairs={{0,14},{2,12},{4,10},{6,8},{8,6},{10,4},{12,2},{14,0},{16,30},{18,... | collective-permute-start | bytes 227336 | tf_op jit(solution)/shard_map/ppermute | solution.py:298
  33.2 0.0 collective-permute-done.2.refs_3_
  33.2 3.0 %collective-permute-start.7 = (bf16[296,128]{1,0:T(8,128)(2,1)S(1)}, bf16[296,128]{1,0:T(8,128)(2,1)S(1)}, u32[]{:S(2)}, u32[]{:S(2)}) collective-permute-start(bf16[296,128]{1,0:T(8,128)(2,1)S(1)} %get-tuple-element.38), channel_id=1, source_target_pairs={{0,16},{2,18},{4,20},{6,22},{8,24},{10,26},{12,28},{14,30},{16,0},... | collective-permute-start | bytes 227336 | tf_op jit(solution)/shard_map/ppermute | solution.py:298
  36.1 0.0 collective-permute-done.3.refs_4_
  36.1 1.3 %collective-permute-start.8 = (bf16[296,128]{1,0:T(8,128)(2,1)S(1)}, bf16[296,128]{1,0:T(8,128)(2,1)S(1)}, u32[]{:S(2)}, u32[]{:S(2)}) collective-permute-start(bf16[296,128]{1,0:T(8,128)(2,1)S(1)} %get-tuple-element.39), channel_id=1, source_target_pairs={{0,18},{2,16},{4,22},{6,20},{8,26},{10,24},{12,30},{14,28},{16,2},... | collective-permute-start | bytes 227336 | tf_op jit(solution)/shard_map/ppermute | solution.py:298
  37.5 0.0 collective-permute-done.4.refs_5_
  37.5 1.5 %collective-permute-start.9 = (bf16[296,128]{1,0:T(8,128)(2,1)S(1)}, bf16[296,128]{1,0:T(8,128)(2,1)S(1)}, u32[]{:S(2)}, u32[]{:S(2)}) collective-permute-start(bf16[296,128]{1,0:T(8,128)(2,1)S(1)} %get-tuple-element.40), channel_id=1, source_target_pairs={{0,20},{2,22},{4,16},{6,18},{8,28},{10,30},{12,24},{14,26},{16,4},... | collective-permute-start | bytes 227336 | tf_op jit(solution)/shard_map/ppermute | solution.py:298
  39.0 0.0 copy-done
  39.0 0.0 copy-done.1
  39.0 3.8 %fetch.1 = (bf16[1024,2304]{1,0:T(8,128)(2,1)S(1)}, bf16[1024,2304]{1,0:T(8,128)(2,1)S(1)}, f32[1024,128]{1,0:T(8,128)S(1)}, f32[1024,128]{1,0:T(8,128)S(1)}, f32[1024,128]{1,0:T(8,128)S(1)}) custom-call(bf16[1024,2304]{1,0:T(8,128)(2,1)} %weights_far.1, bf16[1024,2304]{1,0:T(8,128)(2,1)} %moment_far.1, f32[8,128]{1,0:T(8,128)S(1)} %bitcast.5, ...), custom_call_target="tpu_custom_call" | custom-call | tf_op jit(solution)/shard_map/fetch/pallas_call | solution.py:302
  42.8 0.0 collective-permute-done.5.refs_6_
  42.8 0.0 collective-permute-done.6.refs_7_
  42.8 0.6 %collective-permute-done.7.refs_8_ = bf16[296,128]{1,0:T(8,128)(2,1)S(1)} collective-permute-done((bf16[296,128]{1,0:T(8,128)(2,1)S(1)}, bf16[296,128]{1,0:T(8,128)(2,1)S(1)}, u32[]{:S(2)}, u32[]{:S(2)}) %collective-permute-start.7) | collective-permute-done | bytes 75808 | tf_op jit(solution)/shard_map/ppermute | solution.py:298
  43.4 3.0 %collective-permute-done.8.refs_9_ = bf16[296,128]{1,0:T(8,128)(2,1)S(1)} collective-permute-done((bf16[296,128]{1,0:T(8,128)(2,1)S(1)}, bf16[296,128]{1,0:T(8,128)(2,1)S(1)}, u32[]{:S(2)}, u32[]{:S(2)}) %collective-permute-start.8) | collective-permute-done | bytes 75808 | tf_op jit(solution)/shard_map/ppermute | solution.py:298
  46.4 0.7 %collective-permute-done.9.refs_10_ = bf16[296,128]{1,0:T(8,128)(2,1)S(1)} collective-permute-done((bf16[296,128]{1,0:T(8,128)(2,1)S(1)}, bf16[296,128]{1,0:T(8,128)(2,1)S(1)}, u32[]{:S(2)}, u32[]{:S(2)}) %collective-permute-start.9) | collective-permute-done | bytes 75808 | tf_op jit(solution)/shard_map/ppermute | solution.py:298
  47.0 0.6 %square.1 = (f32[2,128]{1,0:T(2,128)S(1)}, s32[2,128]{1,0:T(2,128)S(1)}) custom-call(bf16[296,128]{1,0:T(8,128)(2,1)S(1)} %get-tuple-element.30.refs_0_, bf16[296,128]{1,0:T(8,128)(2,1)S(1)} %collective-permute-done.refs_1_, bf16[296,128]{1,0:T(8,128)(2,1)S(1)} %collective-permute-done.1.refs_2_, bf16[296,128]{1,0:T(8,128)(2,1)S(1)} %collective-permute-done.2.refs_3_, ...), custom_call_target="tpu_custom_call" | custom-call | flops 301989888 | bytes 1179648 | tf_op jit(solution)/shard_map/square/pallas_call | solution.py:316
  47.7 0.1 collective-permute-start.15
  47.8 3.2 %moment.1 = (f32[1024,2304]{1,0:T(8,128)S(1)}, bf16[1024,2304]{1,0:T(8,128)(2,1)}) custom-call(bf16[296,128]{1,0:T(8,128)(2,1)S(1)} %get-tuple-element.30.refs_0_, bf16[296,128]{1,0:T(8,128)(2,1)S(1)} %collective-permute-done.refs_1_, bf16[296,128]{1,0:T(8,128)(2,1)S(1)} %collective-permute-done.1.refs_2_, ...), custom_call_target="tpu_custom_call" | custom-call | flops 1207959552 | bytes 4718592 | tf_op jit(solution)/shard_map/moment/pallas_call | solution.py:329
  50.9 0.0 collective-permute-done.15.other_ref
  51.0 3.6 %weights.1 = (bf16[1024,2304]{1,0:T(8,128)(2,1)}, f32[8,128]{1,0:T(8,128)}) custom-call(f32[1024,2304]{1,0:T(8,128)S(1)} %get-tuple-element.48.first_ref, bf16[1024,2304]{1,0:T(8,128)(2,1)S(1)} %get-tuple-element.49.weights_ref, f32[2,128]{1,0:T(2,128)S(1)} %get-tuple-element.50.mine_ref, f32[2,128]{1,0:T(2,128)S(1)} %collective-permute-done.15.other_ref, ...), custom_call_target="tpu_custom_call" | custom-call | tf_op jit(solution)/shard_map/weights/pallas_call | solution.py:346
Async XLA Ops:
  0.6 38.3 %copy-start = (f32[1024]{0:T(1024)S(1)}, f32[1024]{0:T(1024)}, u32[]{:S(2)}) copy-start(f32[1024]{0:T(1024)} %param.14) | copy-start | bytes 12292
  0.6 38.3 %copy-start.1 = (s32[1024]{0:T(1024)S(1)}, s32[1024]{0:T(1024)}, u32[]{:S(2)}) copy-start(s32[1024]{0:T(1024)} %param.15) | copy-start | bytes 12292
  6.6 11.8 %collective-permute-start = (bf16[296,128]{1,0:T(8,128)(2,1)S(1)}, bf16[296,128]{1,0:T(8,128)(2,1)S(1)}, u32[]{:S(2)}, u32[]{:S(2)}) collective-permute-start(bf16[296,128]{1,0:T(8,128)(2,1)S(1)} %get-tuple-element.31), channel_id=1, source_target_pairs={{0,2},{2,0},{4,6},{6,4},{8,10},{10,8},{12,14},{14,12},{16,18},{18,... | collective-permute-start | bytes 227336 | tf_op jit(solution)/shard_map/ppermute | solution.py:298
  9.6 11.1 %collective-permute-start.1 = (bf16[296,128]{1,0:T(8,128)(2,1)S(1)}, bf16[296,128]{1,0:T(8,128)(2,1)S(1)}, u32[]{:S(2)}, u32[]{:S(2)}) collective-permute-start(bf16[296,128]{1,0:T(8,128)(2,1)S(1)} %get-tuple-element.32), channel_id=1, source_target_pairs={{0,4},{2,6},{4,0},{6,2},{8,12},{10,14},{12,8},{14,10},{16,20},{18,... | collective-permute-start | bytes 227336 | tf_op jit(solution)/shard_map/ppermute | solution.py:298
  11.1 12.0 %collective-permute-start.10 = (bf16[296,128]{1,0:T(8,128)(2,1)S(1)}, bf16[296,128]{1,0:T(8,128)(2,1)S(1)}, u32[]{:S(2)}, u32[]{:S(2)}) collective-permute-start(bf16[296,128]{1,0:T(8,128)(2,1)S(1)} %get-tuple-element.41), channel_id=1, source_target_pairs={{0,22},{2,20},{4,18},{6,16},{8,30},{10,28},{12,26},{14,24},{16,6},... | collective-permute-start | bytes 227336 | tf_op jit(solution)/shard_map/ppermute | solution.py:298
  13.6 11.9 %collective-permute-start.11 = (bf16[296,128]{1,0:T(8,128)(2,1)S(1)}, bf16[296,128]{1,0:T(8,128)(2,1)S(1)}, u32[]{:S(2)}, u32[]{:S(2)}) collective-permute-start(bf16[296,128]{1,0:T(8,128)(2,1)S(1)} %get-tuple-element.42), channel_id=1, source_target_pairs={{0,24},{2,26},{4,28},{6,30},{8,16},{10,18},{12,20},{14,22},{16,8},... | collective-permute-start | bytes 227336 | tf_op jit(solution)/shard_map/ppermute | solution.py:298
  15.0 10.6 %collective-permute-start.12 = (bf16[296,128]{1,0:T(8,128)(2,1)S(1)}, bf16[296,128]{1,0:T(8,128)(2,1)S(1)}, u32[]{:S(2)}, u32[]{:S(2)}) collective-permute-start(bf16[296,128]{1,0:T(8,128)(2,1)S(1)} %get-tuple-element.43), channel_id=1, source_target_pairs={{0,26},{2,24},{4,30},{6,28},{8,18},{10,16},{12,22},{14,20},{16,10}... | collective-permute-start | bytes 227336 | tf_op jit(solution)/shard_map/ppermute | solution.py:298
  18.4 10.4 %collective-permute-start.13 = (bf16[296,128]{1,0:T(8,128)(2,1)S(1)}, bf16[296,128]{1,0:T(8,128)(2,1)S(1)}, u32[]{:S(2)}, u32[]{:S(2)}) collective-permute-start(bf16[296,128]{1,0:T(8,128)(2,1)S(1)} %get-tuple-element.44), channel_id=1, source_target_pairs={{0,28},{2,30},{4,24},{6,26},{8,20},{10,22},{12,16},{14,18},{16,12}... | collective-permute-start | bytes 227336 | tf_op jit(solution)/shard_map/ppermute | solution.py:298
  20.7 9.7 %collective-permute-start.14 = (bf16[296,128]{1,0:T(8,128)(2,1)S(1)}, bf16[296,128]{1,0:T(8,128)(2,1)S(1)}, u32[]{:S(2)}, u32[]{:S(2)}) collective-permute-start(bf16[296,128]{1,0:T(8,128)(2,1)S(1)} %get-tuple-element.45), channel_id=1, source_target_pairs={{0,30},{2,28},{4,26},{6,24},{8,22},{10,20},{12,18},{14,16},{16,14}... | collective-permute-start | bytes 227336 | tf_op jit(solution)/shard_map/ppermute | solution.py:298
  23.1 10.1 %collective-permute-start.2 = (bf16[296,128]{1,0:T(8,128)(2,1)S(1)}, bf16[296,128]{1,0:T(8,128)(2,1)S(1)}, u32[]{:S(2)}, u32[]{:S(2)}) collective-permute-start(bf16[296,128]{1,0:T(8,128)(2,1)S(1)} %get-tuple-element.33), channel_id=1, source_target_pairs={{0,6},{2,4},{4,2},{6,0},{8,14},{10,12},{12,10},{14,8},{16,22},{18,... | collective-permute-start | bytes 227336 | tf_op jit(solution)/shard_map/ppermute | solution.py:298
  25.6 10.6 %collective-permute-start.3 = (bf16[296,128]{1,0:T(8,128)(2,1)S(1)}, bf16[296,128]{1,0:T(8,128)(2,1)S(1)}, u32[]{:S(2)}, u32[]{:S(2)}) collective-permute-start(bf16[296,128]{1,0:T(8,128)(2,1)S(1)} %get-tuple-element.34), channel_id=1, source_target_pairs={{0,8},{2,10},{4,12},{6,14},{8,0},{10,2},{12,4},{14,6},{16,24},{18,... | collective-permute-start | bytes 227336 | tf_op jit(solution)/shard_map/ppermute | solution.py:298
  25.6 11.9 %collective-permute-start.4 = (bf16[296,128]{1,0:T(8,128)(2,1)S(1)}, bf16[296,128]{1,0:T(8,128)(2,1)S(1)}, u32[]{:S(2)}, u32[]{:S(2)}) collective-permute-start(bf16[296,128]{1,0:T(8,128)(2,1)S(1)} %get-tuple-element.35), channel_id=1, source_target_pairs={{0,10},{2,8},{4,14},{6,12},{8,2},{10,0},{12,6},{14,4},{16,26},{18,... | collective-permute-start | bytes 227336 | tf_op jit(solution)/shard_map/ppermute | solution.py:298
  28.8 14.0 %collective-permute-start.5 = (bf16[296,128]{1,0:T(8,128)(2,1)S(1)}, bf16[296,128]{1,0:T(8,128)(2,1)S(1)}, u32[]{:S(2)}, u32[]{:S(2)}) collective-permute-start(bf16[296,128]{1,0:T(8,128)(2,1)S(1)} %get-tuple-element.36), channel_id=1, source_target_pairs={{0,12},{2,14},{4,8},{6,10},{8,4},{10,6},{12,0},{14,2},{16,28},{18,... | collective-permute-start | bytes 227336 | tf_op jit(solution)/shard_map/ppermute | solution.py:298
  30.4 12.4 %collective-permute-start.6 = (bf16[296,128]{1,0:T(8,128)(2,1)S(1)}, bf16[296,128]{1,0:T(8,128)(2,1)S(1)}, u32[]{:S(2)}, u32[]{:S(2)}) collective-permute-start(bf16[296,128]{1,0:T(8,128)(2,1)S(1)} %get-tuple-element.37), channel_id=1, source_target_pairs={{0,14},{2,12},{4,10},{6,8},{8,6},{10,4},{12,2},{14,0},{16,30},{18,... | collective-permute-start | bytes 227336 | tf_op jit(solution)/shard_map/ppermute | solution.py:298
  33.2 10.2 %collective-permute-start.7 = (bf16[296,128]{1,0:T(8,128)(2,1)S(1)}, bf16[296,128]{1,0:T(8,128)(2,1)S(1)}, u32[]{:S(2)}, u32[]{:S(2)}) collective-permute-start(bf16[296,128]{1,0:T(8,128)(2,1)S(1)} %get-tuple-element.38), channel_id=1, source_target_pairs={{0,16},{2,18},{4,20},{6,22},{8,24},{10,26},{12,28},{14,30},{16,0},... | collective-permute-start | bytes 227336 | tf_op jit(solution)/shard_map/ppermute | solution.py:298
  36.1 10.3 %collective-permute-start.8 = (bf16[296,128]{1,0:T(8,128)(2,1)S(1)}, bf16[296,128]{1,0:T(8,128)(2,1)S(1)}, u32[]{:S(2)}, u32[]{:S(2)}) collective-permute-start(bf16[296,128]{1,0:T(8,128)(2,1)S(1)} %get-tuple-element.39), channel_id=1, source_target_pairs={{0,18},{2,16},{4,22},{6,20},{8,26},{10,24},{12,30},{14,28},{16,2},... | collective-permute-start | bytes 227336 | tf_op jit(solution)/shard_map/ppermute | solution.py:298
  37.5 9.6 %collective-permute-start.9 = (bf16[296,128]{1,0:T(8,128)(2,1)S(1)}, bf16[296,128]{1,0:T(8,128)(2,1)S(1)}, u32[]{:S(2)}, u32[]{:S(2)}) collective-permute-start(bf16[296,128]{1,0:T(8,128)(2,1)S(1)} %get-tuple-element.40), channel_id=1, source_target_pairs={{0,20},{2,22},{4,16},{6,18},{8,28},{10,30},{12,24},{14,26},{16,4},... | collective-permute-start | bytes 227336 | tf_op jit(solution)/shard_map/ppermute | solution.py:298
  47.7 3.3 %collective-permute-start.15 = (f32[2,128]{1,0:T(2,128)S(1)}, f32[2,128]{1,0:T(2,128)S(1)}, u32[]{:S(2)}, u32[]{:S(2)}) collective-permute-start(f32[2,128]{1,0:T(2,128)S(1)} %get-tuple-element.50.mine_ref), channel_id=1, source_target_pairs={{0,1},{1,0},{2,3},{3,2},{4,5},{5,4},{6,7},{7,6},{8,9},{9,8},{10,11... | collective-permute-start | bytes 3080 | tf_op jit(solution)/shard_map/ppermute | solution.py:328

commit v3 on v2

v3 whole, which is shorter than its diff:
```python
import functools

import jax
import jax.numpy as jnp
from jax import lax
from jax.experimental import pallas as pl
from jax.experimental.pallas import tpu as pltpu
from jax.sharding import PartitionSpec as P


LANES = 128
MIB = 1 << 20
VMEM = pl.BlockSpec(memory_space=pltpu.VMEM)
SMEM = pl.BlockSpec(memory_space=pltpu.SMEM)
ANY = pl.BlockSpec(memory_space=pl.ANY)
F32, BF16, I32 = jnp.float32, jnp.bfloat16, jnp.int32


REST_FLOPS = 4 * 10**10


def iota(shape, axis):
    return lax.broadcasted_iota(I32, shape, axis)


def name_rows(slots):
    return -(-2 * (slots // LANES) // 8) * 8


def col_step(half):
    return 2 * LANES if half % (2 * LANES) == 0 else LANES


def spread(turned, first, count, onehot):
    for t in range(turned.shape[0]):
        hit = turned[t : t + 1, :] == iota((count, LANES), 0) + first
        onehot[:, t * LANES : (t + 1) * LANES] = jnp.where(hit, 1.0, 0.0).astype(BF16)


def fill(outs, first, cap, slots, half, names, onehot, buf, chunks, ready):
    base = half // LANES * cap
    groups = slots // LANES
    sub, at = iota(names.shape, 0), iota(names.shape, 1)
    place = (lax.rem(sub, groups) * LANES + at) // cap
    for d, out in enumerate(outs):
        out[base:, :] = jnp.where(place == first + d, names, 0.0).astype(BF16)
    for i, (c, step) in enumerate(chunks):
        ready(i)
        got = jnp.dot(onehot[...], buf[:, c : c + step], preferred_element_type=F32).astype(BF16)
        for d, out in enumerate(outs):
            for t in range(step // LANES):
                row = (c // LANES + t) * cap
                out[row : row + cap, :] = got[d * cap : (d + 1) * cap, t * LANES : (t + 1) * LANES]


def chunks_of(half):
    first = (half // LANES + 1) // 2 * LANES
    return (0, first), (first, half - first)


def far_kernel(
    owners, cap, me_ref, counts_far, slot_far, rows_far, grads_far, *rest
):
    outs, rest = rest[: owners // 2], rest[owners // 2 :]
    grads_ref, turned_ref, names_ref, onehot, counts_ref, slot_ref, rows_ref, sems, small = rest
    _, half = grads_ref.shape
    slots = owners * cap
    chunks = chunks_of(half)
    copies = [
        pltpu.make_async_copy(
            grads_far.at[:, pl.ds(c, step)], grads_ref.at[:, pl.ds(c, step)], sems.at[i]
        )
        for i, (c, step) in enumerate(chunks)
    ]
    arrivals = [
        pltpu.make_async_copy(far, ref, small.at[i])
        for i, (far, ref) in enumerate(
            ((slot_far, slot_ref), (rows_far, rows_ref), (counts_far, counts_ref))
        )
    ]
    for copy in arrivals + copies:
        copy.start()
    for copy in arrivals:
        copy.wait()
    me = me_ref[0]
    groups = slots // LANES
    turned = jnp.bitwise_xor(slot_ref[...], me * cap)
    turned_ref[...] = turned
    spread(turned, slots // 2, slots // 2, onehot)
    lane = iota((1, slots), 1)
    owner, within = lane // cap, lax.rem(lane, cap)
    live = jnp.zeros((1, slots), I32)
    for o in range(owners):
        live = jnp.where((owner == o) & (within < counts_ref[0, o]), 1, live)
    rows = rows_ref[...]
    high = (rows // LANES + 1) * live
    low = lax.rem(rows, LANES) * live
    digits = jnp.concatenate(
        [high.astype(F32), low.astype(F32), jnp.zeros((6, slots), F32)], axis=0
    ).astype(BF16)
    turn = jnp.where(
        iota((slots, slots), 0) == jnp.bitwise_xor(iota((slots, slots), 1), me * cap), 1.0, 0.0
    ).astype(BF16)
    digits = jnp.dot(digits, turn, preferred_element_type=F32)
    pad = name_rows(slots) - 2 * groups
    names = [digits[0:1, g * LANES : (g + 1) * LANES] for g in range(groups)]
    names += [digits[1:2, g * LANES : (g + 1) * LANES] for g in range(groups)]
    if pad:
        names.append(jnp.zeros((pad, LANES), F32))
    names = jnp.concatenate(names, axis=0)
    names_ref[...] = names
    fill(
        outs, owners // 2, cap, slots, half, names, onehot, grads_ref, chunks,
        lambda i: copies[i].wait(),
    )


def rest_kernel(owners, cap, turned_ref, names_ref, grads_ref, steps_ref, *rest):
    outs, (rate_ref, fix_ref, onehot) = rest[: owners // 2], rest[owners // 2 :]
    steps = (steps_ref[...] + 1).astype(F32)
    rate = 0.01 / (1.0 - jnp.exp(steps * jnp.log(jnp.float32(0.9))))
    fix = 1.0 / (1.0 - jnp.exp(steps * jnp.log(jnp.float32(0.95))))
    rate_ref[...] = rate
    fix_ref[...] = fix
    half = grads_ref.shape[1]
    slots = owners * cap
    spread(turned_ref[...], 0, slots // 2, onehot)
    fill(
        outs, 0, cap, slots, half, names_ref[...], onehot, grads_ref, chunks_of(half),
        lambda i: None,
    )


def eye():
    return iota((LANES, LANES), 0) == iota((LANES, LANES), 1)


def to_column(line):
    return jnp.sum(jnp.where(eye(), line, 0.0), axis=1, keepdims=True)


def to_line(column):
    return jnp.sum(jnp.where(eye(), column, 0.0), axis=0, keepdims=True)


def gather_columns(blocks, cap, c, step):
    parts = []
    for t in range(step // LANES):
        at = (c // LANES + t) * cap
        parts.append(jnp.concatenate([b[at : at + cap, :] for b in blocks], axis=0))
    return jnp.concatenate(parts, axis=1) if len(parts) > 1 else parts[0]


def square_kernel(owners, cap, half, *refs):
    blocks = refs[:owners]
    squares_ref, names_ref, columns_ref, same = refs[owners:]
    slots = owners * cap
    groups = slots // LANES
    step = col_step(half)
    base = half // LANES * cap
    names = blocks[0][base:, :].astype(F32)
    for d in range(1, owners):
        names = names + blocks[d][base:, :].astype(F32)
    row = (names[0:groups, :] - 1.0) * LANES + names[groups : 2 * groups, :]
    names_ref[...] = row.astype(I32)
    for g in range(groups):
        column = jnp.broadcast_to(to_column(row[g : g + 1, :]), (LANES, LANES))
        columns_ref[g * LANES : (g + 1) * LANES, :] = column
        for h in range(groups):
            hit = column == row[h : h + 1, :]
            same[g * LANES : (g + 1) * LANES, h * LANES : (h + 1) * LANES] = jnp.where(
                hit, 1.0, 0.0
            ).astype(BF16)
    total = None
    for c in range(0, half, step):
        got = jnp.dot(
            same[...], gather_columns(blocks, cap, c, step), preferred_element_type=F32
        )
        for t in range(step // LANES):
            x = got[:, t * LANES : (t + 1) * LANES]
            total = x * x if total is None else total + x * x
    for g in range(groups):
        column = jnp.sum(total[g * LANES : (g + 1) * LANES, :], axis=1, keepdims=True)
        squares_ref[g : g + 1, :] = to_line(column)


def moment_kernel(owners, cap, *refs):
    blocks, names_ref, moment_ref = refs[:owners], refs[owners], refs[owners + 1]
    first_ref, new_ref, touched_ref, place, keep, staged, sems = refs[owners + 2 :]
    rows, half = moment_ref.shape
    slots = owners * cap
    step = col_step(half)
    for g in range(slots // LANES):
        hit = names_ref[g : g + 1, :] == iota((rows, LANES), 0)
        place[:, g * LANES : (g + 1) * LANES] = jnp.where(hit, 1.0, 0.0).astype(BF16)
    count = jnp.dot(place[...], jnp.ones((slots, LANES), BF16), preferred_element_type=F32)
    keep[...] = jnp.where(count > 0.0, 0.9, 1.0)
    touched_ref[...] = count.astype(BF16)
    copies = []
    block = min(rows, 2 * LANES)
    for c in range(0, half, step):
        got = gather_columns(blocks, cap, c, step)
        for r in range(0, rows, block):
            part = slice(r, r + block)
            grad = jnp.dot(place[part, :], got, preferred_element_type=F32)
            for t in range(step // LANES):
                at = slice(c + t * LANES, c + (t + 1) * LANES)
                first = keep[part, :] * moment_ref[part, at].astype(F32)
                first = first + 0.1 * grad[:, t * LANES : (t + 1) * LANES]
                first_ref[part, at] = first
                staged[part, at] = first.astype(BF16)
        at = pl.ds(c, step)
        copy = pltpu.make_async_copy(staged.at[:, at], new_ref.at[:, at], sems.at[c // step])
        copy.start()
        copies.append(copy)
    for copy in copies:
        copy.wait()


def ready_kernel(weights_ref, kept_ref):
    rows, half = weights_ref.shape
    strip = 16

    @pl.loop(0, rows // strip)
    def _(i):
        part = pl.ds(pl.multiple_of(i * strip, strip), strip)
        for c in range(0, half, LANES):
            at = slice(c, c + LANES)
            kept_ref[part, at] = 0.999 * weights_ref[part, at].astype(F32)


def weights_kernel(
    width, first_ref, weights_ref, kept_ref, touched_ref, mine_ref, other_ref, columns_ref,
    rate_ref, fix_ref, scale_ref, new_ref, new_scale_ref, staged, rates, sems,
):
    rows, half = first_ref.shape
    slots = columns_ref.shape[0]
    lines = rows // LANES
    square = mine_ref[...] + other_ref[...]
    most = [jnp.full((LANES, LANES), -1.0, F32)] * lines
    for g in range(slots // LANES):
        column = jnp.broadcast_to(to_column(square[g : g + 1, :]), (LANES, LANES))
        named = columns_ref[g * LANES : (g + 1) * LANES, :]
        for i in range(lines):
            hit = named == (iota((LANES, LANES), 1) + i * LANES).astype(F32)
            most[i] = jnp.maximum(most[i], jnp.where(hit, column, -1.0))
    most = jnp.concatenate([jnp.max(x, axis=0, keepdims=True) for x in most], axis=0)
    scale = scale_ref[...]
    second = jnp.where(most >= 0.0, 0.95 * scale + 0.05 * (most / width), scale)
    new_scale_ref[...] = second
    rate = rate_ref[...] / (jnp.sqrt(second * fix_ref[...]) + 1e-08)
    for i in range(lines):
        column = to_column(rate[i : i + 1, :])
        rates[i * LANES : (i + 1) * LANES, :] = jnp.broadcast_to(column, (LANES, LANES))
    copies = []
    strip = 16
    for i in range(lines):
        for r in range(i * LANES, (i + 1) * LANES, strip):
            part = slice(r, r + strip)
            rate = rates[part, :]
            touched = touched_ref[part, :] > 0
            for c in range(0, half, LANES):
                at = slice(c, c + LANES)
                new = (kept_ref[part, at] - rate * first_ref[part, at]).astype(BF16)
                staged[part, at] = jnp.where(touched, new, weights_ref[part, at])
        part = pl.ds(i * LANES, LANES)
        copy = pltpu.make_async_copy(staged.at[part, :], new_ref.at[part, :], sems.at[i])
        copy.start()
        copies.append(copy)
    for copy in copies:
        copy.wait()


def near(x):
    return pltpu.with_memory_space_constraint(x, pltpu.VMEM)


def far(x):
    return pltpu.with_memory_space_constraint(x, pltpu.HBM)


def params(limit):
    return pltpu.CompilerParams(vmem_limit_bytes=limit * MIB)


def shards(token_grads, token_slot, slot_rows, counts, weights, moment, row_scale, row_steps):
    owners = lax.axis_size("vocab")
    halves = lax.axis_size("width")
    slots = slot_rows.shape[1]
    cap = slots // owners
    tokens, half = token_grads.shape
    rows = weights.shape[0]
    assert owners & (owners - 1) == 0 and cap & (cap - 1) == 0
    assert rows % LANES == 0 and tokens % LANES == 0 and slots % LANES == 0 and half % LANES == 0
    me = lax.axis_index("vocab").astype(I32).reshape(1)
    height = half // LANES * cap + name_rows(slots)
    step = col_step(half)
    block = jax.ShapeDtypeStruct((height, LANES), BF16)
    cost = pl.CostEstimate(
        flops=slots * tokens * half, bytes_accessed=tokens * half * 2, transcendentals=0
    )
    *upper, grads_near, turned, digits = pl.pallas_call(
        functools.partial(far_kernel, owners, cap),
        out_shape=[block] * (owners // 2)
        + [
            pltpu.VMEM((tokens, half), BF16),
            pltpu.VMEM((tokens // LANES, LANES), I32),
            pltpu.VMEM((name_rows(slots), LANES), F32),
        ],
        in_specs=[SMEM, ANY, ANY, ANY, ANY],
        out_specs=[VMEM] * (owners // 2 + 3),
        scratch_shapes=[
            pltpu.VMEM((slots // 2, tokens), BF16),
            pltpu.SMEM((1, owners), I32),
            pltpu.VMEM((tokens // LANES, LANES), I32),
            pltpu.VMEM((1, slots), I32),
            pltpu.SemaphoreType.DMA((2,)),
            pltpu.SemaphoreType.DMA((3,)),
        ],
        compiler_params=params(12),
        cost_estimate=cost,
        name="far",
    )(
        me, far(counts), far(token_slot.reshape(tokens // LANES, LANES)), far(slot_rows),
        far(token_grads),
    )
    lined = jax.ShapeDtypeStruct((rows // LANES, LANES), F32)
    *lower, rate, fix = pl.pallas_call(
        functools.partial(rest_kernel, owners, cap),
        out_shape=[block] * (owners // 2) + [lined] * 2,
        in_specs=[VMEM] * 4,
        out_specs=[VMEM] * (owners // 2 + 2),
        scratch_shapes=[pltpu.VMEM((slots // 2, tokens), BF16)],
        compiler_params=params(12),
        cost_estimate=pl.CostEstimate(flops=REST_FLOPS, bytes_accessed=0, transcendentals=0),
        name="rest",
    )(
        near(turned), near(digits), near(grads_near), row_steps.reshape(rows // LANES, LANES),
    )
    outgoing = list(lower) + list(upper)
    received = {0: outgoing[0]}
    for d in range(1, owners):
        received[d] = lax.ppermute(outgoing[d], "vocab", [(s, s ^ d) for s in range(owners)])
    blocks = [received[d] for d in range(owners)]
    sloted = (slots // LANES, LANES)
    squares, names, name_columns = pl.pallas_call(
        functools.partial(square_kernel, owners, cap, half),
        out_shape=[
            jax.ShapeDtypeStruct(sloted, F32),
            jax.ShapeDtypeStruct(sloted, I32),
            pltpu.VMEM((slots, LANES), F32),
        ],
        in_specs=[VMEM] * owners,
        out_specs=[VMEM] * 3,
        scratch_shapes=[pltpu.VMEM((slots, slots), BF16)],
        compiler_params=params(10),
        cost_estimate=pl.CostEstimate(
            flops=2 * slots * slots * half, bytes_accessed=slots * half * 2, transcendentals=0
        ),
        name="square",
    )(*blocks)
    other = lax.ppermute(squares, "width", [(s, halves - 1 - s) for s in range(halves)])
    kept = pl.pallas_call(
        ready_kernel,
        out_shape=pltpu.VMEM((rows, half), F32),
        in_specs=[VMEM],
        out_specs=VMEM,
        compiler_params=params(2),
        cost_estimate=pl.CostEstimate(flops=2 * rows * half, bytes_accessed=0, transcendentals=0),
        name="ready",
    )(near(weights))
    first, new_moment, touched = pl.pallas_call(
        functools.partial(moment_kernel, owners, cap),
        out_shape=[
            pltpu.VMEM((rows, half), F32),
            jax.ShapeDtypeStruct((rows, half), BF16),
            pltpu.VMEM((rows, LANES), BF16),
        ],
        in_specs=[VMEM] * (owners + 2),
        out_specs=[VMEM, ANY, VMEM],
        scratch_shapes=[
            pltpu.VMEM((rows, slots), BF16),
            pltpu.VMEM((rows, LANES), F32),
            pltpu.VMEM((rows, half), BF16),
            pltpu.SemaphoreType.DMA((half // step,)),
        ],
        compiler_params=params(16),
        cost_estimate=pl.CostEstimate(
            flops=2 * slots * rows * half, bytes_accessed=2 * rows * half, transcendentals=0
        ),
        name="moment",
    )(*blocks, names, near(moment))
    new_weights, new_scale = pl.pallas_call(
        functools.partial(weights_kernel, halves * half),
        out_shape=[jax.ShapeDtypeStruct((rows, half), BF16), lined],
        in_specs=[VMEM] * 10,
        out_specs=[ANY, VMEM],
        scratch_shapes=[
            pltpu.VMEM((rows, half), BF16),
            pltpu.VMEM((rows, LANES), F32),
            pltpu.SemaphoreType.DMA((rows // LANES,)),
        ],
        compiler_params=params(10),
        name="weights",
    )(
        near(first), near(weights), near(kept), near(touched), squares, other, near(name_columns),
        rate, fix, row_scale.reshape(rows // LANES, LANES),
    )
    return new_weights, new_moment, new_scale.reshape(rows)


def solution(mesh):
    return jax.shard_map(
        shards,
        mesh=mesh,
        in_specs=(
            P("vocab", "width"),
            P("vocab"),
            P("vocab", None),
            P("vocab", None),
            P("vocab", "width"),
            P("vocab", "width"),
            P("vocab"),
            P("vocab"),
        ),
        out_specs=(P("vocab", "width"), P("vocab", "width"), P("vocab")),
        check_vma=False,
    )
```

time: 54.7 us -> 51.8 us (0.947)
  the two profiles are of different devices: /device:TPU:0 before, /device:TPU:9 now
where the time goes in v3:
time: 51.8 us; the launch traced here: 51.7 us
  starting transfers between devices  26.9 us (52%)
  Pallas kernels  12.2 us (24%)
  waiting for transfers between devices  11.8 us (23%)
  between operations  0.75 us (1%)
    ppermute x15, starting transfers between devices, shards(): lax.ppermute(outgoing[d], 'vocab', [(s, s ^ d) for s in range(owners)])  24.9 us
    ppermute x15, waiting for transfers between devices, shards(): lax.ppermute(outgoing[d], 'vocab', [(s, s ^ d) for s in range(owners)])  11.8 us
    pallas_call x1, Pallas kernels, shards(): pl.pallas_call(functools.partial(weights_kernel, halves * half), out_shap...  3.32 us
    pallas_call x1, Pallas kernels, shards(): pl.pallas_call(functools.partial(moment_kernel, owners, cap), out_shape=[...  3.16 us
    pallas_call x1, Pallas kernels, shards(): pl.pallas_call(functools.partial(far_kernel, owners, cap), out_shape=[blo...  3.12 us
    ppermute x1, starting transfers between devices, shards(): lax.ppermute(squares, 'width', [(s, halves - 1 - s) for s in range(halves)])  1.91 us
    pallas_call x1, Pallas kernels, shards(): pl.pallas_call(ready_kernel, out_shape=pltpu.VMEM((rows, half), F32), in_...  1.11 us
  transfers between devices with their start and end apart: 16, of which 5 were waited for; matrix products, arithmetic and copies ran while one was open for 0% of the time, Pallas kernels for 8%

profile of v3, /device:TPU:9, one launch (start us, length us, event | category | flops | bytes accessed | tf_op | source)
XLA Modules:
  0.0 51.7 jit_solution(11210011861965510493)
XLA Ops:
  0.6 0.0 copy-start.1
  0.6 0.0 slice-start
  0.7 3.1 %far.1 = (bf16[296,128]{1,0:T(8,128)(2,1)S(1)}, bf16[296,128]{1,0:T(8,128)(2,1)S(1)}, bf16[296,128]{1,0:T(8,128)(2,1)S(1)}, bf16[296,128]{1,0:T(8,128)(2,1)S(1)}...) custom-call(s32[1]{0:T(128)} %bitcast.me_ref, ...), custom_call_target="tpu_custom_call" | custom-call | flops 603979776 | bytes 4718592 | tf_op jit(solution)/shard_map/far/pallas_call | solution.py:302
  3.8 0.0 copy-done.1
  3.8 0.0 slice-start.1
  3.8 0.9 %rest.1 = (bf16[296,128]{1,0:T(8,128)(2,1)S(1)}, bf16[296,128]{1,0:T(8,128)(2,1)S(1)}, bf16[296,128]{1,0:T(8,128)(2,1)S(1)}, bf16[296,128]{1,0:T(8,128)(2,1)S(1)...) custom-call(s32[8,128]{1,0:T(8,128)S(1)} %get-tuple-element.32.turne, ...), custom_call_target="tpu_custom_call" | custom-call | flops 40000000000 | tf_op jit(solution)/shard_map/rest/pallas_call | solution.py:328
  4.7 1.3 %collective-permute-start = (bf16[296,128]{1,0:T(8,128)(2,1)S(1)}, bf16[296,128]{1,0:T(8,128)(2,1)S(1)}, u32[]{:S(2)}, u32[]{:S(2)}) collective-permute-start(bf16[296,128]{1,0:T(8,128)(2,1)S(1)} %get-tuple-element.36), channel_id=1, source_target_pairs={{0,2},{2,0},{4,6},{6,4},{8,10},{10,8},{12,14},{14,12},{16,18},{18,... | collective-permute-start | bytes 227336 | tf_op jit(solution)/shard_map/ppermute | solution.py:343
  5.9 1.2 %collective-permute-start.1 = (bf16[296,128]{1,0:T(8,128)(2,1)S(1)}, bf16[296,128]{1,0:T(8,128)(2,1)S(1)}, u32[]{:S(2)}, u32[]{:S(2)}) collective-permute-start(bf16[296,128]{1,0:T(8,128)(2,1)S(1)} %get-tuple-element.37), channel_id=1, source_target_pairs={{0,4},{2,6},{4,0},{6,2},{8,12},{10,14},{12,8},{14,10},{16,20},{18,... | collective-permute-start | bytes 227336 | tf_op jit(solution)/shard_map/ppermute | solution.py:343
  7.2 0.2 collective-permute-start.2
  7.4 0.0 collective-permute-start.3
  7.4 2.4 %collective-permute-start.4 = (bf16[296,128]{1,0:T(8,128)(2,1)S(1)}, bf16[296,128]{1,0:T(8,128)(2,1)S(1)}, u32[]{:S(2)}, u32[]{:S(2)}) collective-permute-start(bf16[296,128]{1,0:T(8,128)(2,1)S(1)} %get-tuple-element.40), channel_id=1, source_target_pairs={{0,10},{2,8},{4,14},{6,12},{8,2},{10,0},{12,6},{14,4},{16,26},{18,... | collective-permute-start | bytes 227336 | tf_op jit(solution)/shard_map/ppermute | solution.py:343
  9.8 0.0 collective-permute-done.refs_1_
  9.8 1.1 %collective-permute-start.5 = (bf16[296,128]{1,0:T(8,128)(2,1)S(1)}, bf16[296,128]{1,0:T(8,128)(2,1)S(1)}, u32[]{:S(2)}, u32[]{:S(2)}) collective-permute-start(bf16[296,128]{1,0:T(8,128)(2,1)S(1)} %get-tuple-element.41), channel_id=1, source_target_pairs={{0,12},{2,14},{4,8},{6,10},{8,4},{10,6},{12,0},{14,2},{16,28},{18,... | collective-permute-start | bytes 227336 | tf_op jit(solution)/shard_map/ppermute | solution.py:343
  10.9 0.0 collective-permute-done.1.refs_2_
  10.9 1.2 %collective-permute-start.6 = (bf16[296,128]{1,0:T(8,128)(2,1)S(1)}, bf16[296,128]{1,0:T(8,128)(2,1)S(1)}, u32[]{:S(2)}, u32[]{:S(2)}) collective-permute-start(bf16[296,128]{1,0:T(8,128)(2,1)S(1)} %get-tuple-element.42), channel_id=1, source_target_pairs={{0,14},{2,12},{4,10},{6,8},{8,6},{10,4},{12,2},{14,0},{16,30},{18,... | collective-permute-start | bytes 227336 | tf_op jit(solution)/shard_map/ppermute | solution.py:343
  12.1 0.0 collective-permute-done.2.refs_3_
  12.1 2.3 %collective-permute-start.7 = (bf16[296,128]{1,0:T(8,128)(2,1)S(1)}, bf16[296,128]{1,0:T(8,128)(2,1)S(1)}, u32[]{:S(2)}, u32[]{:S(2)}) collective-permute-start(bf16[296,128]{1,0:T(8,128)(2,1)S(1)} %get-tuple-element.43), channel_id=1, source_target_pairs={{0,16},{2,18},{4,20},{6,22},{8,24},{10,26},{12,28},{14,30},{16,0},... | collective-permute-start | bytes 227336 | tf_op jit(solution)/shard_map/ppermute | solution.py:343
  14.4 0.0 collective-permute-done.3.refs_4_
  14.4 1.0 %collective-permute-start.8 = (bf16[296,128]{1,0:T(8,128)(2,1)S(1)}, bf16[296,128]{1,0:T(8,128)(2,1)S(1)}, u32[]{:S(2)}, u32[]{:S(2)}) collective-permute-start(bf16[296,128]{1,0:T(8,128)(2,1)S(1)} %get-tuple-element.44), channel_id=1, source_target_pairs={{0,18},{2,16},{4,22},{6,20},{8,26},{10,24},{12,30},{14,28},{16,2},... | collective-permute-start | bytes 227336 | tf_op jit(solution)/shard_map/ppermute | solution.py:343
  15.4 0.0 collective-permute-done.4.refs_5_
  15.4 3.3 %collective-permute-start.9 = (bf16[296,128]{1,0:T(8,128)(2,1)S(1)}, bf16[296,128]{1,0:T(8,128)(2,1)S(1)}, u32[]{:S(2)}, u32[]{:S(2)}) collective-permute-start(bf16[296,128]{1,0:T(8,128)(2,1)S(1)} %get-tuple-element.45), channel_id=1, source_target_pairs={{0,20},{2,22},{4,16},{6,18},{8,28},{10,30},{12,24},{14,26},{16,4},... | collective-permute-start | bytes 227336 | tf_op jit(solution)/shard_map/ppermute | solution.py:343
  18.7 0.0 collective-permute-done.5.refs_6_
  18.7 0.0 collective-permute-start.10
  18.7 0.0 collective-permute-done.6.refs_7_
  18.7 1.2 %collective-permute-start.11 = (bf16[296,128]{1,0:T(8,128)(2,1)S(1)}, bf16[296,128]{1,0:T(8,128)(2,1)S(1)}, u32[]{:S(2)}, u32[]{:S(2)}) collective-permute-start(bf16[296,128]{1,0:T(8,128)(2,1)S(1)} %get-tuple-element.47), channel_id=1, source_target_pairs={{0,24},{2,26},{4,28},{6,30},{8,16},{10,18},{12,20},{14,22},{16,8},... | collective-permute-start | bytes 227336 | tf_op jit(solution)/shard_map/ppermute | solution.py:343
  20.0 0.0 collective-permute-done.7.refs_8_
  20.0 1.2 %collective-permute-start.12 = (bf16[296,128]{1,0:T(8,128)(2,1)S(1)}, bf16[296,128]{1,0:T(8,128)(2,1)S(1)}, u32[]{:S(2)}, u32[]{:S(2)}) collective-permute-start(bf16[296,128]{1,0:T(8,128)(2,1)S(1)} %get-tuple-element.48), channel_id=1, source_target_pairs={{0,26},{2,24},{4,30},{6,28},{8,18},{10,16},{12,22},{14,20},{16,10}... | collective-permute-start | bytes 227336 | tf_op jit(solution)/shard_map/ppermute | solution.py:343
  21.1 0.0 collective-permute-done.8.refs_9_
  21.1 4.8 %collective-permute-start.13 = (bf16[296,128]{1,0:T(8,128)(2,1)S(1)}, bf16[296,128]{1,0:T(8,128)(2,1)S(1)}, u32[]{:S(2)}, u32[]{:S(2)}) collective-permute-start(bf16[296,128]{1,0:T(8,128)(2,1)S(1)} %get-tuple-element.49), channel_id=1, source_target_pairs={{0,28},{2,30},{4,24},{6,26},{8,20},{10,22},{12,16},{14,18},{16,12}... | collective-permute-start | bytes 227336 | tf_op jit(solution)/shard_map/ppermute | solution.py:343
  25.9 0.3 collective-permute-done.9.refs_10_
  26.3 0.0 slice-start.2
  26.3 0.0 slice-start.3
  26.3 3.7 %collective-permute-start.14 = (bf16[296,128]{1,0:T(8,128)(2,1)S(1)}, bf16[296,128]{1,0:T(8,128)(2,1)S(1)}, u32[]{:S(2)}, u32[]{:S(2)}) collective-permute-start(bf16[296,128]{1,0:T(8,128)(2,1)S(1)} %get-tuple-element.50), channel_id=1, source_target_pairs={{0,30},{2,28},{4,26},{6,24},{8,22},{10,20},{12,18},{14,16},{16,14}... | collective-permute-start | bytes 227336 | tf_op jit(solution)/shard_map/ppermute | solution.py:343
  30.0 0.0 slice-done
  30.0 0.0 slice-done.1
  30.0 1.1 %ready.1.kept_ref = f32[1024,2304]{1,0:T(8,128)S(1)} custom-call(bf16[1024,2304]{1,0:T(8,128)(2,1)S(1)} %bitcast.6), custom_call_target="tpu_custom_call" | custom-call | flops 4718592 | tf_op jit(solution)/shard_map/ready/pallas_call | solution.py:363
  31.1 0.0 copy-start
  31.1 0.0 collective-permute-done.10.refs_11_
  31.1 3.1 %collective-permute-done.11.refs_12_ = bf16[296,128]{1,0:T(8,128)(2,1)S(1)} collective-permute-done((bf16[296,128]{1,0:T(8,128)(2,1)S(1)}, bf16[296,128]{1,0:T(8,128)(2,1)S(1)}, u32[]{:S(2)}, u32[]{:S(2)}) %collective-permute-start.11) | collective-permute-done | bytes 75808 | tf_op jit(solution)/shard_map/ppermute | solution.py:343
  34.3 3.2 %collective-permute-done.12.refs_13_ = bf16[296,128]{1,0:T(8,128)(2,1)S(1)} collective-permute-done((bf16[296,128]{1,0:T(8,128)(2,1)S(1)}, bf16[296,128]{1,0:T(8,128)(2,1)S(1)}, u32[]{:S(2)}, u32[]{:S(2)}) %collective-permute-start.12) | collective-permute-done | bytes 75808 | tf_op jit(solution)/shard_map/ppermute | solution.py:343
  37.5 3.0 %collective-permute-done.13.refs_14_ = bf16[296,128]{1,0:T(8,128)(2,1)S(1)} collective-permute-done((bf16[296,128]{1,0:T(8,128)(2,1)S(1)}, bf16[296,128]{1,0:T(8,128)(2,1)S(1)}, u32[]{:S(2)}, u32[]{:S(2)}) %collective-permute-start.13) | collective-permute-done | bytes 75808 | tf_op jit(solution)/shard_map/ppermute | solution.py:343
  40.5 2.1 %collective-permute-done.14.refs_15_ = bf16[296,128]{1,0:T(8,128)(2,1)S(1)} collective-permute-done((bf16[296,128]{1,0:T(8,128)(2,1)S(1)}, bf16[296,128]{1,0:T(8,128)(2,1)S(1)}, u32[]{:S(2)}, u32[]{:S(2)}) %collective-permute-start.14) | collective-permute-done | bytes 75808 | tf_op jit(solution)/shard_map/ppermute | solution.py:343
  42.6 0.7 %square.1 = (f32[2,128]{1,0:T(2,128)S(1)}, s32[2,128]{1,0:T(2,128)S(1)}, f32[256,128]{1,0:T(8,128)S(1)}) custom-call(bf16[296,128]{1,0:T(8,128)(2,1)S(1)} %get-tuple-element.35.refs_0_, bf16[296,128]{1,0:T(8,128)(2,1)S(1)} %collective-permute-done.refs_1_, bf16[296,128]{1,0:T(8,128)(2,1)S(1)} %collective-permute-done.1.refs_2_, ...), custom_call_target="tpu_custom_call" | custom-call | flops 301989888 | bytes 1179648 | tf_op jit(solution)/shard_map/square/pallas_call | solution.py:346
  43.3 1.9 %collective-permute-start.15 = (f32[2,128]{1,0:T(2,128)S(1)}, f32[2,128]{1,0:T(2,128)S(1)}, u32[]{:S(2)}, u32[]{:S(2)}) collective-permute-start(f32[2,128]{1,0:T(2,128)S(1)} %get-tuple-element.54.mine_ref), channel_id=1, source_target_pairs={{0,1},{1,0},{2,3},{3,2},{4,5},{5,4},{6,7},{7,6},{8,9},{9,8},{10,11... | collective-permute-start | bytes 3080 | tf_op jit(solution)/shard_map/ppermute | solution.py:362
  45.2 0.0 slice-done.2
  45.2 0.0 slice-done.3
  45.2 3.2 %moment.1 = (f32[1024,2304]{1,0:T(8,128)S(1)}, bf16[1024,2304]{1,0:T(8,128)(2,1)}, bf16[1024,128]{1,0:T(8,128)(2,1)S(1)}) custom-call(bf16[296,128]{1,0:T(8,128)(2,1)S(1)} %get-tuple-element.35.refs_0_, bf16[296,128]{1,0:T(8,128)(2,1)S(1)} %collective-permute-done.refs_1_, bf16[296,128]{1,0:T(8,128)(2,1)S(1)} %collective-permute-done.1.refs_2_, ...), custom_call_target="tpu_custom_call" | custom-call | flops 1207959552 | bytes 4718592 | tf_op jit(solution)/shard_map/moment/pallas_call | solution.py:372
  48.4 0.0 collective-permute-done.15.other_ref
  48.4 0.0 copy-done
  48.4 3.3 %weights.1 = (bf16[1024,2304]{1,0:T(8,128)(2,1)}, f32[8,128]{1,0:T(8,128)}) custom-call(f32[1024,2304]{1,0:T(8,128)S(1)} %get-tuple-element.52.first_ref, bf16[1024,2304]{1,0:T(8,128)(2,1)S(1)} %bitcast.6, f32[1024,2304]{1,0:T(8,128)S(1)} %ready.1.kept_ref, bf16[1024,128]{1,0:T(8,128)(2,1)S(1)} %get-tuple-element.53.touched_ref, ...), custom_call_target="tpu_custom_call" | custom-call | tf_op jit(solution)/shard_map/weights/pallas_call | solution.py:393
  (2 shorter events, 0.0 us)
Async XLA Ops:
  0.6 3.2 %copy-start.1 = (s32[1024]{0:T(1024)S(1)}, s32[1024]{0:T(1024)}, u32[]{:S(2)}) copy-start(s32[1024]{0:T(1024)} %param.15) | copy-start | bytes 12292
  0.6 29.4 %slice-start = ((s8[4718592]{0:T(1024)(128)(4,1)}), s8[4194304]{0:T(1024)(128)(4,1)S(1)}, s32[]{:S(2)}) async-start(s8[4718592]{0:T(1024)(128)(4,1)} %bitcast.5), calls=%async_computation | async-start | bytes 8388608
  3.8 26.2 %slice-start.1 = ((s8[4718592]{0:T(1024)(128)(4,1)}), s8[524288]{0:T(1024)(128)(4,1)S(1)}, s32[]{:S(2)}) async-start(s8[4718592]{0:T(1024)(128)(4,1)} %bitcast.5), calls=%async_computation.1 | async-start | bytes 1048576
  4.7 5.1 %collective-permute-start = (bf16[296,128]{1,0:T(8,128)(2,1)S(1)}, bf16[296,128]{1,0:T(8,128)(2,1)S(1)}, u32[]{:S(2)}, u32[]{:S(2)}) collective-permute-start(bf16[296,128]{1,0:T(8,128)(2,1)S(1)} %get-tuple-element.36), channel_id=1, source_target_pairs={{0,2},{2,0},{4,6},{6,4},{8,10},{10,8},{12,14},{14,12},{16,18},{18,... | collective-permute-start | bytes 227336 | tf_op jit(solution)/shard_map/ppermute | solution.py:343
  5.9 5.0 %collective-permute-start.1 = (bf16[296,128]{1,0:T(8,128)(2,1)S(1)}, bf16[296,128]{1,0:T(8,128)(2,1)S(1)}, u32[]{:S(2)}, u32[]{:S(2)}) collective-permute-start(bf16[296,128]{1,0:T(8,128)(2,1)S(1)} %get-tuple-element.37), channel_id=1, source_target_pairs={{0,4},{2,6},{4,0},{6,2},{8,12},{10,14},{12,8},{14,10},{16,20},{18,... | collective-permute-start | bytes 227336 | tf_op jit(solution)/shard_map/ppermute | solution.py:343
  7.2 4.9 %collective-permute-start.2 = (bf16[296,128]{1,0:T(8,128)(2,1)S(1)}, bf16[296,128]{1,0:T(8,128)(2,1)S(1)}, u32[]{:S(2)}, u32[]{:S(2)}) collective-permute-start(bf16[296,128]{1,0:T(8,128)(2,1)S(1)} %get-tuple-element.38), channel_id=1, source_target_pairs={{0,6},{2,4},{4,2},{6,0},{8,14},{10,12},{12,10},{14,8},{16,22},{18,... | collective-permute-start | bytes 227336 | tf_op jit(solution)/shard_map/ppermute | solution.py:343
  7.4 7.1 %collective-permute-start.3 = (bf16[296,128]{1,0:T(8,128)(2,1)S(1)}, bf16[296,128]{1,0:T(8,128)(2,1)S(1)}, u32[]{:S(2)}, u32[]{:S(2)}) collective-permute-start(bf16[296,128]{1,0:T(8,128)(2,1)S(1)} %get-tuple-element.39), channel_id=1, source_target_pairs={{0,8},{2,10},{4,12},{6,14},{8,0},{10,2},{12,4},{14,6},{16,24},{18,... | collective-permute-start | bytes 227336 | tf_op jit(solution)/shard_map/ppermute | solution.py:343
  7.4 8.1 %collective-permute-start.4 = (bf16[296,128]{1,0:T(8,128)(2,1)S(1)}, bf16[296,128]{1,0:T(8,128)(2,1)S(1)}, u32[]{:S(2)}, u32[]{:S(2)}) collective-permute-start(bf16[296,128]{1,0:T(8,128)(2,1)S(1)} %get-tuple-element.40), channel_id=1, source_target_pairs={{0,10},{2,8},{4,14},{6,12},{8,2},{10,0},{12,6},{14,4},{16,26},{18,... | collective-permute-start | bytes 227336 | tf_op jit(solution)/shard_map/ppermute | solution.py:343
  9.8 8.9 %collective-permute-start.5 = (bf16[296,128]{1,0:T(8,128)(2,1)S(1)}, bf16[296,128]{1,0:T(8,128)(2,1)S(1)}, u32[]{:S(2)}, u32[]{:S(2)}) collective-permute-start(bf16[296,128]{1,0:T(8,128)(2,1)S(1)} %get-tuple-element.41), channel_id=1, source_target_pairs={{0,12},{2,14},{4,8},{6,10},{8,4},{10,6},{12,0},{14,2},{16,28},{18,... | collective-permute-start | bytes 227336 | tf_op jit(solution)/shard_map/ppermute | solution.py:343
  10.9 7.8 %collective-permute-start.6 = (bf16[296,128]{1,0:T(8,128)(2,1)S(1)}, bf16[296,128]{1,0:T(8,128)(2,1)S(1)}, u32[]{:S(2)}, u32[]{:S(2)}) collective-permute-start(bf16[296,128]{1,0:T(8,128)(2,1)S(1)} %get-tuple-element.42), channel_id=1, source_target_pairs={{0,14},{2,12},{4,10},{6,8},{8,6},{10,4},{12,2},{14,0},{16,30},{18,... | collective-permute-start | bytes 227336 | tf_op jit(solution)/shard_map/ppermute | solution.py:343
  12.1 7.8 %collective-permute-start.7 = (bf16[296,128]{1,0:T(8,128)(2,1)S(1)}, bf16[296,128]{1,0:T(8,128)(2,1)S(1)}, u32[]{:S(2)}, u32[]{:S(2)}) collective-permute-start(bf16[296,128]{1,0:T(8,128)(2,1)S(1)} %get-tuple-element.43), channel_id=1, source_target_pairs={{0,16},{2,18},{4,20},{6,22},{8,24},{10,26},{12,28},{14,30},{16,0},... | collective-permute-start | bytes 227336 | tf_op jit(solution)/shard_map/ppermute | solution.py:343
  14.4 6.7 %collective-permute-start.8 = (bf16[296,128]{1,0:T(8,128)(2,1)S(1)}, bf16[296,128]{1,0:T(8,128)(2,1)S(1)}, u32[]{:S(2)}, u32[]{:S(2)}) collective-permute-start(bf16[296,128]{1,0:T(8,128)(2,1)S(1)} %get-tuple-element.44), channel_id=1, source_target_pairs={{0,18},{2,16},{4,22},{6,20},{8,26},{10,24},{12,30},{14,28},{16,2},... | collective-permute-start | bytes 227336 | tf_op jit(solution)/shard_map/ppermute | solution.py:343
  15.4 10.8 %collective-permute-start.9 = (bf16[296,128]{1,0:T(8,128)(2,1)S(1)}, bf16[296,128]{1,0:T(8,128)(2,1)S(1)}, u32[]{:S(2)}, u32[]{:S(2)}) collective-permute-start(bf16[296,128]{1,0:T(8,128)(2,1)S(1)} %get-tuple-element.45), channel_id=1, source_target_pairs={{0,20},{2,22},{4,16},{6,18},{8,28},{10,30},{12,24},{14,26},{16,4},... | collective-permute-start | bytes 227336 | tf_op jit(solution)/shard_map/ppermute | solution.py:343
  18.7 12.4 %collective-permute-start.10 = (bf16[296,128]{1,0:T(8,128)(2,1)S(1)}, bf16[296,128]{1,0:T(8,128)(2,1)S(1)}, u32[]{:S(2)}, u32[]{:S(2)}) collective-permute-start(bf16[296,128]{1,0:T(8,128)(2,1)S(1)} %get-tuple-element.46), channel_id=1, source_target_pairs={{0,22},{2,20},{4,18},{6,16},{8,30},{10,28},{12,26},{14,24},{16,6},... | collective-permute-start | bytes 227336 | tf_op jit(solution)/shard_map/ppermute | solution.py:343
  18.7 15.5 %collective-permute-start.11 = (bf16[296,128]{1,0:T(8,128)(2,1)S(1)}, bf16[296,128]{1,0:T(8,128)(2,1)S(1)}, u32[]{:S(2)}, u32[]{:S(2)}) collective-permute-start(bf16[296,128]{1,0:T(8,128)(2,1)S(1)} %get-tuple-element.47), channel_id=1, source_target_pairs={{0,24},{2,26},{4,28},{6,30},{8,16},{10,18},{12,20},{14,22},{16,8},... | collective-permute-start | bytes 227336 | tf_op jit(solution)/shard_map/ppermute | solution.py:343
  20.0 17.5 %collective-permute-start.12 = (bf16[296,128]{1,0:T(8,128)(2,1)S(1)}, bf16[296,128]{1,0:T(8,128)(2,1)S(1)}, u32[]{:S(2)}, u32[]{:S(2)}) collective-permute-start(bf16[296,128]{1,0:T(8,128)(2,1)S(1)} %get-tuple-element.48), channel_id=1, source_target_pairs={{0,26},{2,24},{4,30},{6,28},{8,18},{10,16},{12,22},{14,20},{16,10}... | collective-permute-start | bytes 227336 | tf_op jit(solution)/shard_map/ppermute | solution.py:343
  21.1 19.4 %collective-permute-start.13 = (bf16[296,128]{1,0:T(8,128)(2,1)S(1)}, bf16[296,128]{1,0:T(8,128)(2,1)S(1)}, u32[]{:S(2)}, u32[]{:S(2)}) collective-permute-start(bf16[296,128]{1,0:T(8,128)(2,1)S(1)} %get-tuple-element.49), channel_id=1, source_target_pairs={{0,28},{2,30},{4,24},{6,26},{8,20},{10,22},{12,16},{14,18},{16,12}... | collective-permute-start | bytes 227336 | tf_op jit(solution)/shard_map/ppermute | solution.py:343
  26.3 18.9 %slice-start.2 = ((s8[4718592]{0:T(1024)(128)(4,1)}), s8[4194304]{0:T(1024)(128)(4,1)S(1)}, s32[]{:S(2)}) async-start(s8[4718592]{0:T(1024)(128)(4,1)} %bitcast.7), calls=%async_computation.2 | async-start | bytes 8388608
  26.3 18.9 %slice-start.3 = ((s8[4718592]{0:T(1024)(128)(4,1)}), s8[524288]{0:T(1024)(128)(4,1)S(1)}, s32[]{:S(2)}) async-start(s8[4718592]{0:T(1024)(128)(4,1)} %bitcast.7), calls=%async_computation.3 | async-start | bytes 1048576
  26.3 16.3 %collective-permute-start.14 = (bf16[296,128]{1,0:T(8,128)(2,1)S(1)}, bf16[296,128]{1,0:T(8,128)(2,1)S(1)}, u32[]{:S(2)}, u32[]{:S(2)}) collective-permute-start(bf16[296,128]{1,0:T(8,128)(2,1)S(1)} %get-tuple-element.50), channel_id=1, source_target_pairs={{0,30},{2,28},{4,26},{6,24},{8,22},{10,20},{12,18},{14,16},{16,14}... | collective-permute-start | bytes 227336 | tf_op jit(solution)/shard_map/ppermute | solution.py:343
  31.1 17.3 %copy-start = (f32[1024]{0:T(1024)S(1)}, f32[1024]{0:T(1024)}, u32[]{:S(2)}) copy-start(f32[1024]{0:T(1024)} %param.14) | copy-start | bytes 12292
  43.3 5.1 %collective-permute-start.15 = (f32[2,128]{1,0:T(2,128)S(1)}, f32[2,128]{1,0:T(2,128)S(1)}, u32[]{:S(2)}, u32[]{:S(2)}) collective-permute-start(f32[2,128]{1,0:T(2,128)S(1)} %get-tuple-element.54.mine_ref), channel_id=1, source_target_pairs={{0,1},{1,0},{2,3},{3,2},{4,5},{5,4},{6,7},{7,6},{8,9},{9,8},{10,11... | collective-permute-start | bytes 3080 | tf_op jit(solution)/shard_map/ppermute | solution.py:362
